TPU v7x, 32 devices: a 4x4x1 block of a 4x4x8 slice. The times are simulated.
32 devices in a mesh: dp: 1 (over z), tp: 4 (over y), sp: 8 (over x, core).
Axes of the slice: x: 4, y: 4, z: 1, core: 2. Of those that a mesh axis runs over, the one named last changes fastest.
The devices are a block of a 4x4x8 slice.
Arguments:
- x_in: bfloat16 [8192, 5120], P(('dp', 'sp'), 'tp')
- w_qkv: bfloat16 [5120, 15360], P('sp', 'tp')
- w_out: bfloat16 [5120, 5120], P('sp', 'tp')
- seg_ids: int32 [8192], P(('dp', 'sp'))
Outputs:
- output: bfloat16 [8192, 5120], P(('dp', 'sp'), 'tp')
All inputs are finite; a program needn't handle non-finite values.
Results may differ from a plain program's by a relative error of at most 0.00321.
Values are sent between devices in bfloat16 or wider.
A program may use at most 768 MiB of HBM per device.

v0:
```python
import jax
import jax.numpy as jnp
from jax import lax
from jax.sharding import PartitionSpec as P, NamedSharding

HEAD_DIM = 128
QUERY_BLOCK = 128


def solution(mesh):
    def local_block(x_blk, wqkv_blk, wout_blk, seg_blk):
        n_rows, local_cols = x_blk.shape
        local_heads = local_cols // HEAD_DIM
        n_blocks = n_rows // QUERY_BLOCK
        score_scale = 1.0 / HEAD_DIM ** 0.5
        x_rows = lax.all_gather(x_blk, "tp", axis=1, tiled=True)
        wqkv_cols = lax.all_gather(wqkv_blk, "sp", axis=0, tiled=True)
        qkv_proj = jnp.dot(x_rows, wqkv_cols, preferred_element_type=jnp.float32).astype(jnp.bfloat16)
        qkv_proj = qkv_proj.reshape(n_rows, local_heads, 3, HEAD_DIM)
        query_loc = qkv_proj[:, :, 0].reshape(n_blocks, QUERY_BLOCK, local_heads, HEAD_DIM)
        kv_all = lax.all_gather(qkv_proj[:, :, 1:], "sp", axis=0, tiled=True)
        seg_all = lax.all_gather(seg_blk, "sp", axis=0, tiled=True)
        key_all = kv_all[:, :, 0]
        value_all = kv_all[:, :, 1]
        positions = jnp.arange(kv_all.shape[0], dtype=jnp.int32)
        pos_query = (lax.axis_index("sp") * n_rows + jnp.arange(n_rows, dtype=jnp.int32)).reshape(n_blocks, QUERY_BLOCK)
        seg_query = seg_blk.reshape(n_blocks, QUERY_BLOCK)

        def one_block(block_args):
            query_blk, pos_blk, segq_blk = block_args
            scores = jnp.einsum("qnd,knd->nqk", query_blk, key_all, preferred_element_type=jnp.float32) * score_scale
            allowed = (positions[None, :] <= pos_blk[:, None]) & (seg_all[None, :] == segq_blk[:, None])
            scores = jnp.where(allowed[None], scores, -jnp.inf)
            prob_blk = jax.nn.softmax(scores, axis=-1).astype(jnp.bfloat16)
            return jnp.einsum("nqk,knd->qnd", prob_blk, value_all, preferred_element_type=jnp.float32).astype(jnp.bfloat16)

        context = lax.map(one_block, (query_loc, pos_query, seg_query)).reshape(n_rows, local_cols)
        context_rows = lax.all_gather(context, "tp", axis=1, tiled=True)
        wout_cols = lax.all_gather(wout_blk, "sp", axis=0, tiled=True)
        return jnp.dot(context_rows, wout_cols, preferred_element_type=jnp.float32).astype(jnp.bfloat16)

    row_spec = P(("dp", "sp"), "tp")
    return jax.shard_map(local_block, mesh=mesh, in_specs=(row_spec, P("sp", "tp"), P("sp", "tp"), P(("dp", "sp"))), out_specs=row_spec, check_vma=False)
```

profile of v0, /device:TPU:97, one launch (start us, length us, event | category | flops | bytes accessed | tf_op | source)
XLA Modules:
  0.0 1482.2 jit_solution(783874885169180581)
XLA Ops:
  8.2 103.1 %all-gather.6.cloned.1.call-done = bf16[1024,5120]{1,0:T(8,128)(2,1)} async-done(((bf16[1024,1280]{1,0:T(8,128)(2,1)}), bf16[1024,5120]{1,0:T(8,128)(2,1)}) %all-gather.6.cloned.1.call-update) | async-done | bytes 10485776 | tf_op jit(solution)/shard_map/all_gather | solution.py:16
  111.3 183.2 %all-gather.8.cloned.1.call-done = bf16[5120,3840]{1,0:T(8,128)(2,1)} async-done(((bf16[640,3840]{1,0:T(8,128)(2,1)}), bf16[5120,3840]{1,0:T(8,128)(2,1)}) %all-gather.8.cloned.1.call-update) | async-done | bytes 39321616 | tf_op jit(solution)/shard_map/all_gather | solution.py:17
  294.5 48.9 %convolution_convert_fusion = bf16[1024,3840]{1,0:T(8,128)(2,1)} fusion(bf16[1024,5120]{1,0:T(8,128)(2,1)} %all-gather.6.cloned.1.call-done, bf16[5120,3840]{1,0:T(8,128)(2,1)} %all-gather.8.cloned.1.call-done), kind=kOutput, calls=%fused_computation.27 | convolution fusion | flops 40269250560 | bytes 57671680 | tf_op jit(solution)/shard_map/dot_general | solution.py:18
  381.4 168.7 %all-gather.10.cloned.1.call-done = bf16[8192,10,2,128]{0,3,2,1:T(8,128)(2,1)} async-done(((bf16[1024,10,2,128]{0,3,2,1:T(8,128)(2,1)}), bf16[8192,10,2,128]{0,3,2,1:T(8,128)(2,1)}) %all-gather.10.cloned.1.call-update) | async-done | bytes 41943056 | tf_op jit(solution)/shard_map/all_gather | solution.py:21
  550.0 28.0 %slice_bitcast_fusion = (bf16[8192,10,128]{0,2,1:T(8,128)(2,1)}, bf16[8192,10,128]{0,2,1:T(8,128)(2,1)}) fusion(bf16[8192,10,2,128]{0,3,2,1:T(8,128)(2,1)} %all-gather.10.cloned.1.call-done), kind=kLoop, calls=%fused_computation.25 | loop fusion | bytes 83886080 | tf_op jit(solution)/shard_map/squeeze | solution.py:24
  578.0 26.6 %copy.15 = bf16[8192,10,128]{2,0,1:T(8,128)(2,1)} copy(bf16[8192,10,128]{0,2,1:T(8,128)(2,1)} %get-tuple-element.108) | data formatting | bytes 41943040
  604.7 26.6 %copy.16 = bf16[8192,10,128]{2,0,1:T(8,128)(2,1)} copy(bf16[8192,10,128]{0,2,1:T(8,128)(2,1)} %get-tuple-element.107) | data formatting | bytes 41943040
  631.3 720.1 %while.11 = (s32[]{:T(128)}, bf16[8,128,10,128]{3,1,2,0:T(8,128)(2,1)}, s32[8,128]{1,0:T(8,128)S(1)}, s32[8192]{0:T(1024)S(1)}, s32[8,128]{1,0:T(8,128)S(1)}, /*...) while((s32[]{:T(128)}, ...), condition=%wide.region_3.4_spmd.clone, body=%wide.region_0.3_spmd.clone.sunk | while | flops 5455912960 | bytes 212514928 | solution.py:37
  632.2 20.9 %fusion.38 = f32[10,128,8192]{2,1,0:T(8,128)} fusion(bf16[8192,10,128]{2,0,1:T(8,128)(2,1)} %get-tuple-element.190, bf16[8,128,10,128]{3,1,0,2:T(8,128)(2,1)} %get-tuple-element.189, s32[]{:T(128)} %get-tuple-element.175), kind=kOutput, calls=%fused_computation.15.clone.1 | convolution fusion | flops 2684354560 | bytes 63242752 | tf_op jit(solution)/shard_map/while/body/eval_jaxpr/qnd,knd->nqk/dot_general | solution.py:31
  653.2 46.2 %fusion.41 = (f32[10,128]{1,0:T(8,128)S(1)}, f32[10,128,8192]{2,1,0:T(8,128)}) fusion(f32[10,128,8192]{2,1,0:T(8,128)} %fusion.38, pred[128,8192]{1,0:T(8,128)(4,1)S(1)} %fusion.40), kind=kOutput, calls=%fused_computation.31.clone.1 | output fusion | flops 62922752 | bytes 84939776 | tf_op jit(solution)/shard_map/while/body/eval_jaxpr/sub | solution.py:34
  699.3 22.0 %fusion.42 = bf16[8,128,10,128]{3,1,2,0:T(8,128)(2,1)} fusion(bf16[8,128,10,128]{3,1,2,0:T(8,128)(2,1)} %get-tuple-element.176, s32[]{:T(128)} %get-tuple-element.175, bf16[8192,10,128]{2,0,1:T(8,128)(2,1)} %get-tuple-element.191, f32[10,128,8192]{2,1,0:T(8,128)} %get-tuple-element.164, f32[10,128]{1,0:T(8,128)S(1)} %get-tuple-element.165), kind=kOutput, calls=%fused_computation.14.clone.1 | convolution fusion | flops 2705489920 | bytes 63247872 | tf_op jit(solution)/shard_map/while/body/eval_jaxpr/nqk,knd->qnd/dot_general | solution.py:35
  722.2 20.9 %fusion.38 = f32[10,128,8192]{2,1,0:T(8,128)} fusion(bf16[8192,10,128]{2,0,1:T(8,128)(2,1)} %get-tuple-element.190, bf16[8,128,10,128]{3,1,0,2:T(8,128)(2,1)} %get-tuple-element.189, s32[]{:T(128)} %get-tuple-element.175), kind=kOutput, calls=%fused_computation.15.clone.1 | convolution fusion | flops 2684354560 | bytes 63242752 | tf_op jit(solution)/shard_map/while/body/eval_jaxpr/qnd,knd->nqk/dot_general | solution.py:31
  743.2 46.2 %fusion.41 = (f32[10,128]{1,0:T(8,128)S(1)}, f32[10,128,8192]{2,1,0:T(8,128)}) fusion(f32[10,128,8192]{2,1,0:T(8,128)} %fusion.38, pred[128,8192]{1,0:T(8,128)(4,1)S(1)} %fusion.40), kind=kOutput, calls=%fused_computation.31.clone.1 | output fusion | flops 62922752 | bytes 84939776 | tf_op jit(solution)/shard_map/while/body/eval_jaxpr/sub | solution.py:34
  789.3 22.0 %fusion.42 = bf16[8,128,10,128]{3,1,2,0:T(8,128)(2,1)} fusion(bf16[8,128,10,128]{3,1,2,0:T(8,128)(2,1)} %get-tuple-element.176, s32[]{:T(128)} %get-tuple-element.175, bf16[8192,10,128]{2,0,1:T(8,128)(2,1)} %get-tuple-element.191, f32[10,128,8192]{2,1,0:T(8,128)} %get-tuple-element.164, f32[10,128]{1,0:T(8,128)S(1)} %get-tuple-element.165), kind=kOutput, calls=%fused_computation.14.clone.1 | convolution fusion | flops 2705489920 | bytes 63247872 | tf_op jit(solution)/shard_map/while/body/eval_jaxpr/nqk,knd->qnd/dot_general | solution.py:35
  812.2 20.9 %fusion.38 = f32[10,128,8192]{2,1,0:T(8,128)} fusion(bf16[8192,10,128]{2,0,1:T(8,128)(2,1)} %get-tuple-element.190, bf16[8,128,10,128]{3,1,0,2:T(8,128)(2,1)} %get-tuple-element.189, s32[]{:T(128)} %get-tuple-element.175), kind=kOutput, calls=%fused_computation.15.clone.1 | convolution fusion | flops 2684354560 | bytes 63242752 | tf_op jit(solution)/shard_map/while/body/eval_jaxpr/qnd,knd->nqk/dot_general | solution.py:31
  833.2 46.2 %fusion.41 = (f32[10,128]{1,0:T(8,128)S(1)}, f32[10,128,8192]{2,1,0:T(8,128)}) fusion(f32[10,128,8192]{2,1,0:T(8,128)} %fusion.38, pred[128,8192]{1,0:T(8,128)(4,1)S(1)} %fusion.40), kind=kOutput, calls=%fused_computation.31.clone.1 | output fusion | flops 62922752 | bytes 84939776 | tf_op jit(solution)/shard_map/while/body/eval_jaxpr/sub | solution.py:34
  879.4 22.0 %fusion.42 = bf16[8,128,10,128]{3,1,2,0:T(8,128)(2,1)} fusion(bf16[8,128,10,128]{3,1,2,0:T(8,128)(2,1)} %get-tuple-element.176, s32[]{:T(128)} %get-tuple-element.175, bf16[8192,10,128]{2,0,1:T(8,128)(2,1)} %get-tuple-element.191, f32[10,128,8192]{2,1,0:T(8,128)} %get-tuple-element.164, f32[10,128]{1,0:T(8,128)S(1)} %get-tuple-element.165), kind=kOutput, calls=%fused_computation.14.clone.1 | convolution fusion | flops 2705489920 | bytes 63247872 | tf_op jit(solution)/shard_map/while/body/eval_jaxpr/nqk,knd->qnd/dot_general | solution.py:35
  902.3 20.9 %fusion.38 = f32[10,128,8192]{2,1,0:T(8,128)} fusion(bf16[8192,10,128]{2,0,1:T(8,128)(2,1)} %get-tuple-element.190, bf16[8,128,10,128]{3,1,0,2:T(8,128)(2,1)} %get-tuple-element.189, s32[]{:T(128)} %get-tuple-element.175), kind=kOutput, calls=%fused_computation.15.clone.1 | convolution fusion | flops 2684354560 | bytes 63242752 | tf_op jit(solution)/shard_map/while/body/eval_jaxpr/qnd,knd->nqk/dot_general | solution.py:31
  923.2 46.2 %fusion.41 = (f32[10,128]{1,0:T(8,128)S(1)}, f32[10,128,8192]{2,1,0:T(8,128)}) fusion(f32[10,128,8192]{2,1,0:T(8,128)} %fusion.38, pred[128,8192]{1,0:T(8,128)(4,1)S(1)} %fusion.40), kind=kOutput, calls=%fused_computation.31.clone.1 | output fusion | flops 62922752 | bytes 84939776 | tf_op jit(solution)/shard_map/while/body/eval_jaxpr/sub | solution.py:34
  969.4 22.0 %fusion.42 = bf16[8,128,10,128]{3,1,2,0:T(8,128)(2,1)} fusion(bf16[8,128,10,128]{3,1,2,0:T(8,128)(2,1)} %get-tuple-element.176, s32[]{:T(128)} %get-tuple-element.175, bf16[8192,10,128]{2,0,1:T(8,128)(2,1)} %get-tuple-element.191, f32[10,128,8192]{2,1,0:T(8,128)} %get-tuple-element.164, f32[10,128]{1,0:T(8,128)S(1)} %get-tuple-element.165), kind=kOutput, calls=%fused_computation.14.clone.1 | convolution fusion | flops 2705489920 | bytes 63247872 | tf_op jit(solution)/shard_map/while/body/eval_jaxpr/nqk,knd->qnd/dot_general | solution.py:35
  992.3 20.9 %fusion.38 = f32[10,128,8192]{2,1,0:T(8,128)} fusion(bf16[8192,10,128]{2,0,1:T(8,128)(2,1)} %get-tuple-element.190, bf16[8,128,10,128]{3,1,0,2:T(8,128)(2,1)} %get-tuple-element.189, s32[]{:T(128)} %get-tuple-element.175), kind=kOutput, calls=%fused_computation.15.clone.1 | convolution fusion | flops 2684354560 | bytes 63242752 | tf_op jit(solution)/shard_map/while/body/eval_jaxpr/qnd,knd->nqk/dot_general | solution.py:31
  1013.2 46.2 %fusion.41 = (f32[10,128]{1,0:T(8,128)S(1)}, f32[10,128,8192]{2,1,0:T(8,128)}) fusion(f32[10,128,8192]{2,1,0:T(8,128)} %fusion.38, pred[128,8192]{1,0:T(8,128)(4,1)S(1)} %fusion.40), kind=kOutput, calls=%fused_computation.31.clone.1 | output fusion | flops 62922752 | bytes 84939776 | tf_op jit(solution)/shard_map/while/body/eval_jaxpr/sub | solution.py:34
  1059.4 22.0 %fusion.42 = bf16[8,128,10,128]{3,1,2,0:T(8,128)(2,1)} fusion(bf16[8,128,10,128]{3,1,2,0:T(8,128)(2,1)} %get-tuple-element.176, s32[]{:T(128)} %get-tuple-element.175, bf16[8192,10,128]{2,0,1:T(8,128)(2,1)} %get-tuple-element.191, f32[10,128,8192]{2,1,0:T(8,128)} %get-tuple-element.164, f32[10,128]{1,0:T(8,128)S(1)} %get-tuple-element.165), kind=kOutput, calls=%fused_computation.14.clone.1 | convolution fusion | flops 2705489920 | bytes 63247872 | tf_op jit(solution)/shard_map/while/body/eval_jaxpr/nqk,knd->qnd/dot_general | solution.py:35
  1082.3 20.9 %fusion.38 = f32[10,128,8192]{2,1,0:T(8,128)} fusion(bf16[8192,10,128]{2,0,1:T(8,128)(2,1)} %get-tuple-element.190, bf16[8,128,10,128]{3,1,0,2:T(8,128)(2,1)} %get-tuple-element.189, s32[]{:T(128)} %get-tuple-element.175), kind=kOutput, calls=%fused_computation.15.clone.1 | convolution fusion | flops 2684354560 | bytes 63242752 | tf_op jit(solution)/shard_map/while/body/eval_jaxpr/qnd,knd->nqk/dot_general | solution.py:31
  1103.2 46.2 %fusion.41 = (f32[10,128]{1,0:T(8,128)S(1)}, f32[10,128,8192]{2,1,0:T(8,128)}) fusion(f32[10,128,8192]{2,1,0:T(8,128)} %fusion.38, pred[128,8192]{1,0:T(8,128)(4,1)S(1)} %fusion.40), kind=kOutput, calls=%fused_computation.31.clone.1 | output fusion | flops 62922752 | bytes 84939776 | tf_op jit(solution)/shard_map/while/body/eval_jaxpr/sub | solution.py:34
  1149.4 22.0 %fusion.42 = bf16[8,128,10,128]{3,1,2,0:T(8,128)(2,1)} fusion(bf16[8,128,10,128]{3,1,2,0:T(8,128)(2,1)} %get-tuple-element.176, s32[]{:T(128)} %get-tuple-element.175, bf16[8192,10,128]{2,0,1:T(8,128)(2,1)} %get-tuple-element.191, f32[10,128,8192]{2,1,0:T(8,128)} %get-tuple-element.164, f32[10,128]{1,0:T(8,128)S(1)} %get-tuple-element.165), kind=kOutput, calls=%fused_computation.14.clone.1 | convolution fusion | flops 2705489920 | bytes 63247872 | tf_op jit(solution)/shard_map/while/body/eval_jaxpr/nqk,knd->qnd/dot_general | solution.py:35
  1172.3 20.9 %fusion.38 = f32[10,128,8192]{2,1,0:T(8,128)} fusion(bf16[8192,10,128]{2,0,1:T(8,128)(2,1)} %get-tuple-element.190, bf16[8,128,10,128]{3,1,0,2:T(8,128)(2,1)} %get-tuple-element.189, s32[]{:T(128)} %get-tuple-element.175), kind=kOutput, calls=%fused_computation.15.clone.1 | convolution fusion | flops 2684354560 | bytes 63242752 | tf_op jit(solution)/shard_map/while/body/eval_jaxpr/qnd,knd->nqk/dot_general | solution.py:31
  1193.3 46.2 %fusion.41 = (f32[10,128]{1,0:T(8,128)S(1)}, f32[10,128,8192]{2,1,0:T(8,128)}) fusion(f32[10,128,8192]{2,1,0:T(8,128)} %fusion.38, pred[128,8192]{1,0:T(8,128)(4,1)S(1)} %fusion.40), kind=kOutput, calls=%fused_computation.31.clone.1 | output fusion | flops 62922752 | bytes 84939776 | tf_op jit(solution)/shard_map/while/body/eval_jaxpr/sub | solution.py:34
  1239.4 22.0 %fusion.42 = bf16[8,128,10,128]{3,1,2,0:T(8,128)(2,1)} fusion(bf16[8,128,10,128]{3,1,2,0:T(8,128)(2,1)} %get-tuple-element.176, s32[]{:T(128)} %get-tuple-element.175, bf16[8192,10,128]{2,0,1:T(8,128)(2,1)} %get-tuple-element.191, f32[10,128,8192]{2,1,0:T(8,128)} %get-tuple-element.164, f32[10,128]{1,0:T(8,128)S(1)} %get-tuple-element.165), kind=kOutput, calls=%fused_computation.14.clone.1 | convolution fusion | flops 2705489920 | bytes 63247872 | tf_op jit(solution)/shard_map/while/body/eval_jaxpr/nqk,knd->qnd/dot_general | solution.py:35
  1283.3 46.2 %fusion.41 = (f32[10,128]{1,0:T(8,128)S(1)}, f32[10,128,8192]{2,1,0:T(8,128)}) fusion(f32[10,128,8192]{2,1,0:T(8,128)} %fusion.38, pred[128,8192]{1,0:T(8,128)(4,1)S(1)} %fusion.40), kind=kOutput, calls=%fused_computation.31.clone.1 | output fusion | flops 62922752 | bytes 84939776 | tf_op jit(solution)/shard_map/while/body/eval_jaxpr/sub | solution.py:34
  1329.4 22.0 %fusion.42 = bf16[8,128,10,128]{3,1,2,0:T(8,128)(2,1)} fusion(bf16[8,128,10,128]{3,1,2,0:T(8,128)(2,1)} %get-tuple-element.176, s32[]{:T(128)} %get-tuple-element.175, bf16[8192,10,128]{2,0,1:T(8,128)(2,1)} %get-tuple-element.191, f32[10,128,8192]{2,1,0:T(8,128)} %get-tuple-element.164, f32[10,128]{1,0:T(8,128)S(1)} %get-tuple-element.165), kind=kOutput, calls=%fused_computation.14.clone.1 | convolution fusion | flops 2705489920 | bytes 63247872 | tf_op jit(solution)/shard_map/while/body/eval_jaxpr/nqk,knd->qnd/dot_general | solution.py:35
  1357.5 97.4 %all-gather.12.cloned.1.call-done = bf16[1024,5120]{0,1:T(8,128)(2,1)} async-done(((bf16[1024,1280]{0,1:T(8,128)(2,1)}), bf16[1024,5120]{0,1:T(8,128)(2,1)}) %all-gather.12.cloned.1.call-update) | async-done | bytes 10485776 | tf_op jit(solution)/shard_map/all_gather | solution.py:38
  (40 shorter events, 94.5 us)
Async XLA Ops:
  6.5 104.7 %all-gather.6.cloned.1.call-start = ((), (), s32[]{:S(2)}) async-start(), calls=%async_computation | async-start | bytes 13107200 | tf_op jit(solution)/shard_map/all_gather | solution.py:16
  7.3 287.2 %all-gather.8.cloned.1.call-start = ((), (), s32[]{:S(2)}) async-start(), calls=%async_computation.1 | async-start | bytes 44236800 | tf_op jit(solution)/shard_map/all_gather | solution.py:17
  8.1 541.9 %all-gather.10.cloned.1.call-start = ((), (), s32[]{:S(2)}) async-start(), calls=%async_computation.2 | async-start | bytes 47185920 | tf_op jit(solution)/shard_map/all_gather | solution.py:21
  343.3 17.2 %copy-start = (s32[1024]{0:T(1024)S(1)}, s32[1024]{0:T(1024)}, u32[]{:S(2)}) copy-start(s32[1024]{0:T(1024)} %param.9) | copy-start | bytes 12292
  359.8 997.7 %all-gather.14.cloned.1.call-start = ((), (), s32[]{:S(2)}) async-start(), calls=%async_computation.4 | async-start | bytes 14745600 | tf_op jit(solution)/shard_map/all_gather | solution.py:39
  360.4 1094.5 %all-gather.12.cloned.1.call-start = ((), (), s32[]{:S(2)}) async-start(), calls=%async_computation.3 | async-start | bytes 13107200 | tf_op jit(solution)/shard_map/all_gather | solution.py:38
Sparse Core Ops, SparseCore 0:
  8.9 102.3 all-gather.5
  112.9 181.5 all-gather.7
  359.9 190.0 all-gather.9
  551.5 66.2 all-gather.13
  1357.6 97.3 all-gather.11
where the time goes:
time: 1480 us
  waiting for transfers between devices  555 us (38%)
  matrix products  413 us (28%)
  other arithmetic  377 us (25%)
  local copies, waits for them, and re-layouts  108 us (7%)
  blocking collectives  16 us (1%)
    sub x8, other arithmetic, one_block(): prob_blk = jax.nn.softmax(scores, axis=-1).astype(jnp.bfloat16)  369 us
    all_gather x1, waiting for transfers between devices, local_block(): wqkv_cols = lax.all_gather(wqkv_blk, 'sp', axis=0, tiled=True)  183 us
    dot_general x8, matrix products, one_block(): jnp.einsum('nqk,knd->qnd', prob_blk, value_all, preferred_element_type=jn...  176 us
    all_gather x1, waiting for transfers between devices, local_block(): kv_all = lax.all_gather(qkv_proj[:, :, 1:], 'sp', axis=0, tiled=True)  169 us
    dot_general x8, matrix products, one_block(): jnp.einsum('qnd,knd->nqk', query_blk, key_all, preferred_element_type=jnp...  168 us
    all_gather x1, waiting for transfers between devices, local_block(): x_rows = lax.all_gather(x_blk, 'tp', axis=1, tiled=True)  103 us
    all_gather x1, waiting for transfers between devices, local_block(): context_rows = lax.all_gather(context, 'tp', axis=1, tiled=True)  97.4 us
    unnamed x5, local copies, waits for them, and re-layouts  55.4 us
  transfers between devices with their start and end apart: 5, of which 4 were waited for; matrix products, arithmetic and copies ran while one was open for 55% of the time, Pallas kernels for 0%

commit v1 on v0

v1 whole, which is shorter than its diff:
```python
import functools

import jax
import jax.numpy as jnp
from jax import lax
from jax.experimental import pallas as pl
from jax.experimental.pallas import tpu as pltpu
from jax.sharding import PartitionSpec as P

HEAD_DIM = 128
MESH = pl.DeviceIdType.MESH
ANY = pl.ANY
VMEM_LIMIT = 60 * 1024 * 1024


class Place:
    def __init__(self, n_tp, n_sp):
        self.n_tp, self.n_sp, self.n_x = n_tp, n_sp, n_sp // 2
        self.tp, self.sp = lax.axis_index("tp"), lax.axis_index("sp")
        self.chip, self.core = self.sp // 2, self.sp % 2
        self.sib = self.chip * 2 + 1 - self.core
        self.up, self.down = (self.tp + 1) % n_tp, (self.tp + n_tp - 1) % n_tp
        self.right, self.left = self.at(1, 0), self.at(-1, 0)

    def chip_at(self, r):
        return (self.chip + r + self.n_x) % self.n_x

    def at(self, r, d):
        return self.chip_at(r) * 2 + (self.core if d == 0 else 1 - self.core)

    def barrier(self):
        sem = pltpu.get_barrier_semaphore()
        for j in range(1, self.n_sp):
            pl.semaphore_signal(sem, inc=1, device_id={"sp": (self.sp + j) % self.n_sp}, device_id_type=MESH)
        for peer in (self.up, self.down):
            pl.semaphore_signal(sem, inc=1, device_id={"tp": peer}, device_id_type=MESH)
        pl.semaphore_wait(sem, self.n_sp + 1)


def remote(src, dst, send, recv, **peer):
    return pltpu.make_async_remote_copy(
        src_ref=src, dst_ref=dst, send_sem=send, recv_sem=recv, device_id=peer, device_id_type=MESH
    )


class Ring:
    HALF = (0, 1, 0, 1, 0, 1)

    def __init__(self, axis, me, ahead, behind, far, own, slots, rows, send, recv):
        self.half = (pl.ds(0, rows // 2), pl.ds(rows // 2, rows // 2))
        self.axis, self.me, self.ahead, self.behind, self.far = axis, me, ahead, behind, far
        self.own, self.slots, self.send, self.recv = own, slots, send, recv

    def copy(self, k):
        h = self.half[self.HALF[k]]
        if k in (2, 5):
            src = dst = self.landed(k - 2)
        else:
            src, dst = self.own.at[h], self.slots(self.me).at[h]
        peer = self.ahead if k < 3 else self.behind
        return remote(src, dst, self.send.at[k], self.recv.at[k], **{self.axis: peer})

    def landed(self, k):
        origin = (self.behind, self.behind, self.far, self.ahead, self.ahead, self.far)[k]
        return self.slots(origin).at[self.half[self.HALF[k]]]

    def start(self):
        for k in (0, 3, 1, 4):
            self.copy(k).start()

    def forward(self):
        for k in (0, 3):
            self.copy(k).wait_recv()
            self.copy(k + 2).start()

    def wait(self, *ks):
        for k in ks:
            self.copy(k).wait_recv()

    def drain(self):
        for k in range(6):
            self.copy(k).wait_send()


class WeightGather:
    def __init__(self, p, w_ref, w_all, send, recv, sib_send, sib_recv):
        self.p, self.send, self.recv = p, sib_send, sib_recv
        self.ring = Ring("sp", p.sp, p.right, p.left, p.at(2, 0), w_ref, lambda i: w_all.at[i], w_ref.shape[0],
                         send, recv)
        self.own = remote(w_ref, w_all.at[p.sp], sib_send.at[6], sib_recv.at[6], sp=p.sib)

    def start(self):
        self.ring.start()
        self.own.start()

    def to_sibling(self, k):
        block = self.ring.landed(k)
        return remote(block, block, self.send.at[k], self.recv.at[k], sp=self.p.sib)

    def forward(self):
        self.ring.forward()
        self.share(0, 3)

    def share(self, *ks):
        for k in ks:
            self.to_sibling(k).start()

    def wait_sibling(self, *ks):
        for k in ks:
            self.to_sibling(k).wait_recv()

    def drain(self):
        self.ring.drain()
        self.own.wait_send()
        for k in range(6):
            self.to_sibling(k).wait_send()


def qkv_kernel(n_tp, n_sp, x_ref, w_ref, seg_ref, m_all, skv, sq, seg_all, w_all,
               x_all, acc, qkv, w_tile, local_sem, tile_sem, ring_send, ring_recv, w_sib_send, w_sib_recv,
               seg_send, seg_recv, main_send, main_recv, kv_send, kv_recv, q_send, q_recv, own_sem):
    p = Place(n_tp, n_sp)
    rows, x_cols = x_ref.shape
    w_rows = w_ref.shape[0]
    n_tiles, _, tile = acc.shape
    head = 3 * HEAD_DIM
    n_shared = 2 * n_tiles - n_sp
    parts = n_sp // n_shared
    q_rows = rows // parts
    m_tile = min(rows, 256)
    p.barrier()

    x_own = pltpu.make_async_copy(x_ref, x_all.at[p.tp], local_sem.at[0])
    x_own.start()
    seg_own = pltpu.make_async_copy(seg_ref, seg_all.at[p.sp], local_sem.at[1])
    seg_own.start()
    x_ring = Ring("tp", p.tp, p.up, p.down, (p.tp + 2) % n_tp, x_ref, lambda i: x_all.at[i], rows,
                  ring_send.at[0], ring_recv.at[0])
    weight = WeightGather(p, w_ref, w_all, ring_send.at[1], ring_recv.at[1], w_sib_send, w_sib_recv)
    weight.start()
    x_ring.start()
    seg_copies = []
    for j in range(1, n_sp):
        copy = remote(seg_ref, seg_all.at[p.sp], seg_send.at[j - 1], seg_recv.at[j - 1], sp=(p.sp + j) % n_sp)
        copy.start()
        seg_copies.append(copy)

    def tile_load(w_src, t, slot):
        return pltpu.make_async_copy(
            w_src.at[:, pl.ds(pl.multiple_of(t * tile, tile), tile)], w_tile.at[slot], tile_sem.at[slot])

    def product(shard, m, slot):
        r = pl.ds(pl.multiple_of(m * m_tile, m_tile), m_tile)
        c = pl.ds(pl.multiple_of((shard % 2) * w_rows, w_rows), w_rows)
        return r, jnp.dot(x_all[shard // 2, r, c], w_tile[slot], preferred_element_type=jnp.float32)

    def accumulate(w_src, shard, first=False):
        tile_load(w_src, 0, 0).start()

        @pl.loop(0, n_tiles)
        def _(t):
            slot = t % 2
            tile_load(w_src, t, slot).wait()

            @pl.when(t + 1 < n_tiles)
            def _():
                tile_load(w_src, t + 1, 1 - slot).start()

            @pl.loop(0, rows // m_tile)
            def _(m):
                r, d = product(shard, m, slot)
                if first:
                    acc[t, r] = d
                else:
                    acc[t, r] += d

    x_ring.forward()
    weight.forward()
    x_ring.wait(1, 4, 2, 5)
    x_own.wait()
    accumulate(w_ref, p.sp, first=True)
    weight.own.wait_recv()
    accumulate(w_all.at[p.sib], p.sib)
    weight.ring.wait(1, 4)
    weight.share(1, 4)
    accumulate(w_all.at[p.left], p.left)
    accumulate(w_all.at[p.right], p.right)
    weight.wait_sibling(0, 1)
    accumulate(w_all.at[p.at(-1, 1)], p.at(-1, 1))
    weight.wait_sibling(3, 4)
    accumulate(w_all.at[p.at(1, 1)], p.at(1, 1))
    weight.ring.wait(2, 5)
    weight.share(2, 5)
    accumulate(w_all.at[p.at(2, 0)], p.at(2, 0))
    weight.wait_sibling(2, 5)

    last = p.at(2, 1)
    offsets = (2, 1, -1, None, 0)
    order = [n_tiles - 1 if r is None else p.chip_at(r) for r in offsets]
    pending = []
    tile_load(w_all.at[last], order[0], 0).start()
    for i, (r, t) in enumerate(zip(offsets, order)):
        slot = i % 2
        tile_load(w_all.at[last], t, slot).wait()
        if i + 1 < n_tiles:
            tile_load(w_all.at[last], order[i + 1], 1 - slot).start()

        @pl.loop(0, rows // m_tile)
        def _(m):
            rr, d = product(last, m, slot)
            qkv[t, rr] = (acc[t, rr] + d).astype(qkv.dtype)

        if r is not None:
            for d in (0, 1):
                core = p.core if d == 0 else 1 - p.core
                src = qkv.at[t, :, pl.ds(pl.multiple_of(core * head, head), head)]
                if r == 0 and d == 0:
                    copy = pltpu.make_async_copy(src, m_all.at[p.sp], own_sem.at[0])
                else:
                    j = (r % 4) * 2 + d
                    copy = remote(src, m_all.at[p.sp], main_send.at[j], main_recv.at[j], sp=p.at(r, d))
                copy.start()
                pending.append((copy, r == 0 and d == 0))
            continue
        for r2 in (2, 1, -1, 0):
            base = (p.chip_at(r2) * 2 // parts) * head
            kv_src = qkv.at[t, :, pl.ds(pl.multiple_of(base + HEAD_DIM, HEAD_DIM), 2 * HEAD_DIM)]
            if r2 == 0:
                copy = pltpu.make_async_copy(kv_src, skv.at[p.sp], own_sem.at[1])
                copy.start()
                pending.append((copy, True))
                copy = remote(kv_src, skv.at[p.sp], kv_send.at[0], kv_recv.at[0], sp=p.sib)
            else:
                copy = remote(kv_src, skv.at[p.sp], kv_send.at[r2 % 4], kv_recv.at[r2 % 4], sp=p.at(r2, 0))
            copy.start()
            if r2 == 0:
                pending.append((copy, False))
            else:
                pending.append((copy, None))
            for d in (0, 1):
                dst = p.at(r2, d)
                q_src = qkv.at[t, pl.ds(pl.multiple_of((dst % parts) * q_rows, q_rows), q_rows),
                               pl.ds(pl.multiple_of(base, HEAD_DIM), HEAD_DIM)]
                if r2 == 0 and d == 0:
                    copy = pltpu.make_async_copy(q_src, sq.at[p.sp], own_sem.at[2])
                else:
                    j = (r2 % 4) * 2 + d
                    copy = remote(q_src, sq.at[p.sp], q_send.at[j], q_recv.at[j], sp=dst)
                copy.start()
                pending.append((copy, r2 == 0 and d == 0))

    relays = []
    for r in (1, -1, 2):
        k = r % 4
        arrived = skv.at[p.at(-r, 0)]
        remote(arrived, arrived, kv_send.at[k], kv_recv.at[k], sp=p.at(r, 0)).wait_recv()
        relay = remote(arrived, arrived, kv_send.at[3 + k], kv_recv.at[3 + k], sp=p.sib)
        relay.start()
        relays.append(relay)
    for copy, local in pending:
        if local:
            copy.wait()
        else:
            copy.wait_send()
            if local is False:
                copy.wait_recv()
    for relay in relays:
        relay.wait()
    for copy in seg_copies:
        copy.wait()
    seg_own.wait()
    x_ring.drain()
    weight.drain()


def attention_kernel(scale, parts, n_main, tab, m_ref, skv_ref, sq_ref, o_ref, so_ref, vt, svt, exps, tops):
    step = pl.program_id(0)
    seq = m_ref.shape[0]
    q_tile = o_ref.shape[0]
    k_tile = 2 * q_tile
    n_bounds = tab.shape[0] - 1
    coef = scale * 1.4426950408889634
    lowest = -0.7 * float(jnp.finfo(jnp.float32).max)

    @pl.when(step == 0)
    def _():
        @pl.loop(0, seq // k_tile)
        def _(j):
            r = pl.ds(pl.multiple_of(j * k_tile, k_tile), k_tile)
            vt[j] = m_ref[r, 2 * HEAD_DIM:].T
            svt[j] = skv_ref[r, HEAD_DIM:].T

    def doc_start(row):
        start = row * 0
        for d in range(n_bounds):
            start = jnp.where(row >= tab[d], tab[d], start)
        return start

    def attend(q, k_ref, k_col, vt_ref, row0, out):
        row = row0 + lax.broadcasted_iota(jnp.int32, (1, q_tile), 1)
        start = doc_start(row)
        first = doc_start(row0) // k_tile
        diagonal = row0 // k_tile
        clear = (doc_start(row0 + q_tile - 1) + k_tile - 1) // k_tile
        clear = jnp.minimum(clear, diagonal)

        def body(masked, j, carry):
            top, total = carry
            r = pl.ds(pl.multiple_of(j * k_tile, k_tile), k_tile)
            s = lax.dot_general(k_ref[r, k_col:k_col + HEAD_DIM], q, (((1,), (1,)), ((), ())),
                                preferred_element_type=jnp.float32)
            if masked:
                key = j * k_tile + lax.broadcasted_iota(jnp.int32, s.shape, 0)
                s = jnp.where((key >= start) & (key <= row), s, lowest)
            new = jnp.maximum(top, jnp.max(s, axis=0, keepdims=True))
            e = jnp.exp2((s - new) * coef)
            exps[j] = e
            tops[j] = new
            total = total * jnp.exp2((top - new) * coef) + jnp.sum(e, axis=0, keepdims=True)
            return new, total

        def weigh(j, o):
            share = jnp.exp2((tops[j] - top) * coef) / total
            prob = (exps[j] * share).astype(jnp.bfloat16)
            return o + jnp.dot(vt_ref[j], prob, preferred_element_type=jnp.float32)

        carry = (jnp.full((1, q_tile), lowest, jnp.float32), jnp.zeros((1, q_tile), jnp.float32))
        carry = lax.fori_loop(first, clear, functools.partial(body, True), carry)
        carry = lax.fori_loop(clear, diagonal, functools.partial(body, False), carry)
        top, total = body(True, diagonal, carry)
        o = lax.fori_loop(first, diagonal + 1, weigh, jnp.zeros((HEAD_DIM, q_tile), jnp.float32))
        out[...] = o.T.astype(out.dtype)

    @pl.when(step < n_main)
    def _():
        row0 = step * q_tile
        q = m_ref[pl.ds(pl.multiple_of(row0, q_tile), q_tile), :HEAD_DIM]
        attend(q, m_ref, HEAD_DIM, vt, row0, o_ref)

    @pl.when(step >= n_main)
    def _():
        i = step - n_main
        row0 = (i * parts + tab[n_bounds]) * q_tile
        q = sq_ref[pl.ds(pl.multiple_of(i * q_tile, q_tile), q_tile), :]
        attend(q, skv_ref, 0, svt, row0, so_ref)


def out_kernel(n_tp, n_sp, o_ref, so_ref, w_ref, y_ref, ctx, w_all, acc, local_sem, w_send, w_recv, w_sib_send,
               w_sib_recv, o_send, o_recv, s_send, s_recv, c_send, c_recv):
    p = Place(n_tp, n_sp)
    n_x = p.n_x
    _, rows, local = ctx.shape
    w_rows = w_ref.shape[0]
    n_shared = local // HEAD_DIM - n_sp
    parts = n_sp // n_shared
    q_rows = rows // parts
    m_tile = min(rows, 256)
    pair = 2 * HEAD_DIM
    p.barrier()

    w_own = pltpu.make_async_copy(w_ref, w_all.at[p.sp], local_sem.at[0])
    w_own.start()

    def head_copy(r, d):
        dst = p.at(r, d)
        src = o_ref.at[pl.ds(pl.multiple_of(dst * rows, rows), rows)]
        to = ctx.at[p.tp, :, pl.ds(pl.multiple_of(p.sp * HEAD_DIM, HEAD_DIM), HEAD_DIM)]
        if r == 0 and d == 0:
            return pltpu.make_async_copy(src, to, local_sem.at[1])
        j = (r % 4) * 2 + d
        return remote(src, to, o_send.at[j], o_recv.at[j], sp=dst)

    def shared_copy(r, d):
        dst = p.at(r, d)
        src = so_ref.at[pl.ds(pl.multiple_of(dst * q_rows, q_rows), q_rows)]
        to = ctx.at[p.tp, pl.ds(pl.multiple_of((p.sp % parts) * q_rows, q_rows), q_rows),
                    pl.ds(pl.multiple_of((n_sp + p.sp // parts) * HEAD_DIM, HEAD_DIM), HEAD_DIM)]
        if r == 0 and d == 0:
            return pltpu.make_async_copy(src, to, local_sem.at[2])
        j = (r % 4) * 2 + d
        return remote(src, to, s_send.at[j], s_recv.at[j], sp=dst)

    peers = [(r, d) for r in (0, 1, -1, 2) for d in (0, 1)]
    for r, d in peers:
        head_copy(r, d).start()
    for r, d in peers:
        shared_copy(r, d).start()
    weight = WeightGather(p, w_ref, w_all, w_send, w_recv, w_sib_send, w_sib_recv)
    weight.start()

    def ring(i, column):
        c = pl.ds(pl.multiple_of(column, pair), pair)
        return Ring("tp", p.tp, p.up, p.down, (p.tp + 2) % n_tp, ctx.at[p.tp, :, c], lambda j: ctx.at[j, :, c], rows,
                    c_send.at[i], c_recv.at[i])

    def wait_in(copy, local):
        if local:
            copy.wait()
        else:
            copy.wait_recv()

    rings = []
    for i, r in enumerate((0, 1, -1, 2)):
        for d in (0, 1):
            wait_in(head_copy(r, d), r == 0 and d == 0)
        rings.append(ring(i, p.chip_at(-r) * pair))
        rings[-1].start()
    for r, d in peers:
        wait_in(shared_copy(r, d), r == 0 and d == 0)
    rings.append(ring(n_x, n_sp * HEAD_DIM))
    rings[-1].start()
    for c in rings:
        c.forward()
    weight.forward()
    weight.ring.wait(1, 4)
    weight.share(1, 4)
    for c in rings:
        c.wait(1, 4)
    w_own.wait()
    weight.own.wait_recv()
    weight.wait_sibling(0, 1, 3, 4)

    def block(j, step):
        @pl.loop(0, rows // m_tile)
        def _(m):
            r = pl.ds(pl.multiple_of(m * m_tile, m_tile), m_tile)
            d = jnp.dot(ctx[j, r, :w_rows], w_all[2 * j], preferred_element_type=jnp.float32)
            d += jnp.dot(ctx[j, r, w_rows:], w_all[2 * j + 1], preferred_element_type=jnp.float32)
            if step == 0:
                acc[r] = d
            elif step < n_tp - 1:
                acc[r] += d
            else:
                y_ref[r] = (acc[r] + d).astype(y_ref.dtype)

    turn = (p.chip + n_x - p.tp) % n_x
    far = turn // 2
    block((p.tp + far * (1 - turn % 2)) % n_tp, 0)
    block((p.tp + 1 + 2 * far) % n_tp, 1)
    weight.ring.wait(2, 5)
    weight.share(2, 5)
    weight.wait_sibling(2, 5)
    block((p.tp + far * (turn - 2) + (1 - far) * 3) % n_tp, 2)
    for c in rings:
        c.wait(2, 5)
    block((p.tp + 2) % n_tp, 3)

    for c in rings:
        c.drain()
    weight.drain()
    for r, d in peers:
        if not (r == 0 and d == 0):
            head_copy(r, d).wait_send()
            shared_copy(r, d).wait_send()


def solution(mesh):
    n_tp, n_sp = mesh.shape["tp"], mesh.shape["sp"]
    dma = pltpu.SemaphoreType.DMA
    hbm = pl.BlockSpec(memory_space=ANY)

    def params(collective_id):
        return pltpu.CompilerParams(collective_id=collective_id, has_side_effects=True, vmem_limit_bytes=VMEM_LIMIT)

    def local_block(x_blk, wqkv_blk, wout_blk, seg_blk):
        rows, x_cols = x_blk.shape
        w_rows, n_cols = wqkv_blk.shape
        head = 3 * HEAD_DIM
        heads = n_cols // head
        local = heads * HEAD_DIM
        n_shared = heads - n_sp
        parts = n_sp // n_shared
        q_rows = rows // parts
        tile = 2 * head
        n_tiles = n_cols // tile
        seq = n_sp * rows
        bf16 = x_blk.dtype
        n_docs = 4

        seg = seg_blk.reshape(rows // 128, 128)
        m_all, skv, sq, seg_all, _ = pl.pallas_call(
            functools.partial(qkv_kernel, n_tp, n_sp),
            out_shape=(
                jax.ShapeDtypeStruct((n_sp, rows, head), bf16),
                jax.ShapeDtypeStruct((n_sp, rows, 2 * HEAD_DIM), bf16),
                jax.ShapeDtypeStruct((n_sp, q_rows, HEAD_DIM), bf16),
                jax.ShapeDtypeStruct((n_sp,) + seg.shape, seg.dtype),
                jax.ShapeDtypeStruct((n_sp, w_rows, n_cols), bf16),
            ),
            in_specs=[hbm] * 3,
            out_specs=(hbm,) * 5,
            scratch_shapes=[
                pltpu.VMEM((n_tp, rows, x_cols), bf16),
                pltpu.VMEM((n_tiles, rows, tile), jnp.float32),
                pltpu.VMEM((n_tiles, rows, tile), bf16),
                pltpu.VMEM((2, w_rows, tile), bf16),
                dma((2,)), dma((2,)), dma((2, 6)), dma((2, 6)), dma((7,)), dma((7,)),
                dma((n_sp - 1,)), dma((n_sp - 1,)), dma((8,)), dma((8,)), dma((7,)), dma((7,)), dma((8,)), dma((8,)),
                dma((3,)),
            ],
            compiler_params=params(0),
            name="qkv",
        )(x_blk, wqkv_blk, seg)

        starts = jnp.sum((seg_all.reshape(1, seq) < jnp.arange(1, n_docs, dtype=seg_all.dtype)[:, None]).astype(jnp.int32),
                         axis=1)
        table = jnp.concatenate([starts, (lax.axis_index("sp") % parts).astype(jnp.int32)[None]])
        n_main = seq // q_rows

        def whole(shape):
            return pl.BlockSpec(shape, lambda i, t: (0, 0), pipeline_mode=pl.Buffered(1))

        o_main, o_shared = pl.pallas_call(
            functools.partial(attention_kernel, 1.0 / HEAD_DIM ** 0.5, parts, n_main),
            out_shape=(jax.ShapeDtypeStruct((seq, HEAD_DIM), bf16), jax.ShapeDtypeStruct((seq // parts, HEAD_DIM), bf16)),
            grid_spec=pltpu.PrefetchScalarGridSpec(
                num_scalar_prefetch=1,
                grid=(n_main + n_main // parts,),
                in_specs=[whole((seq, head)), whole((seq, 2 * HEAD_DIM)), whole((seq // parts, HEAD_DIM))],
                out_specs=(pl.BlockSpec((q_rows, HEAD_DIM), lambda i, t: (jnp.minimum(i, n_main - 1), 0)),
                           pl.BlockSpec((q_rows, HEAD_DIM), lambda i, t: (jnp.maximum(i - n_main, 0), 0))),
                scratch_shapes=[pltpu.VMEM((seq // (2 * q_rows), HEAD_DIM, 2 * q_rows), bf16)] * 2 + [
                    pltpu.VMEM((seq // (2 * q_rows), 2 * q_rows, q_rows), jnp.float32),
                    pltpu.VMEM((seq // (2 * q_rows), 1, q_rows), jnp.float32),
                ],
            ),
            compiler_params=pltpu.CompilerParams(dimension_semantics=("arbitrary",), vmem_limit_bytes=VMEM_LIMIT),
            name="attention",
        )(table, m_all.reshape(seq, head), skv.reshape(seq, 2 * HEAD_DIM), sq.reshape(seq // parts, HEAD_DIM))

        wo_rows, wo_cols = wout_blk.shape
        n_rings = local // (2 * HEAD_DIM)
        return pl.pallas_call(
            functools.partial(out_kernel, n_tp, n_sp),
            out_shape=jax.ShapeDtypeStruct((rows, wo_cols), bf16),
            in_specs=[hbm] * 3,
            out_specs=pl.BlockSpec(memory_space=pltpu.VMEM),
            scratch_shapes=[
                pltpu.VMEM((n_tp, rows, local), bf16),
                pltpu.VMEM((n_sp, wo_rows, wo_cols), bf16),
                pltpu.VMEM((rows, wo_cols), jnp.float32),
                dma((3,)), dma((6,)), dma((6,)), dma((7,)), dma((7,)),
                dma((8,)), dma((8,)), dma((8,)), dma((8,)), dma((n_rings, 6)), dma((n_rings, 6)),
            ],
            compiler_params=params(1),
            name="out",
        )(o_main, o_shared, wout_blk)

    row_spec = P(("dp", "sp"), "tp")
    return jax.shard_map(
        local_block, mesh=mesh, in_specs=(row_spec, P("sp", "tp"), P("sp", "tp"), P(("dp", "sp"))),
        out_specs=row_spec, check_vma=False)
```

time: 1480 us -> 506 us (0.34)
  waiting for transfers between devices: 555 us -> 0 us
  Pallas kernels: 0 us -> 496 us
  matrix products: 413 us -> 0 us
  other arithmetic: 377 us -> 1.68 us
  local copies, waits for them, and re-layouts: 108 us -> 3.4 us
  blocking collectives: 16 us -> 0 us
    all_gather x5 -> x0, waiting for transfers between devices: 552 us -> none  [the longest x1 183 us: local_block(): wqkv_cols = lax.all_gather(wqkv_blk, 'sp', axis=0, tiled=True)]
    pallas_call x0 -> x3, Pallas kernels: none -> 496 us  [the longest x1 280 us: local_block(): pl.pallas_call(functools.partial(qkv_kernel, n_tp, n_sp), out_shape=(jax....]
    dot_general x18 -> x0, matrix products: 413 us -> none  [the longest x8 176 us: one_block(): jnp.einsum('nqk,knd->qnd', prob_blk, value_all, preferred_element_type=jn...]
    sub x8 -> x0, other arithmetic: 369 us -> none  [one_block(): prob_blk = jax.nn.softmax(scores, axis=-1).astype(jnp.bfloat16)]
    unnamed x5 -> x1, local copies, waits for them, and re-layouts: 55.4 us -> 3.4 us
    squeeze x1 -> x0, local copies, waits for them, and re-layouts: 28 us -> none  [local_block(): value_all = kv_all[:, :, 1]]
    all_gather x1 -> x0, blocking collectives: 16 us -> none  [local_block(): seg_all = lax.all_gather(seg_blk, 'sp', axis=0, tiled=True)]
  transfers between devices with their start and end apart: 5 -> 0, of which waited for: 4 -> 0; matrix products, arithmetic and copies ran while one was open for 55% -> 0% of each run, Pallas kernels for 0% -> 0%
where the time goes in v1:
time: 506 us; the launch traced here: 501 us
  Pallas kernels  496 us (98%)
    pallas_call x1, Pallas kernels, local_block(): pl.pallas_call(functools.partial(qkv_kernel, n_tp, n_sp), out_shape=(jax....  280 us
    pallas_call x1, Pallas kernels, local_block(): pl.pallas_call(functools.partial(attention_kernel, 1.0 / HEAD_DIM ** 0.5,...  109 us
    pallas_call x1, Pallas kernels, local_block(): pl.pallas_call(functools.partial(out_kernel, n_tp, n_sp), out_shape=jax.S...  106 us

profile of v1, /device:TPU:97, one launch (start us, length us, event | category | flops | bytes accessed | tf_op | source)
XLA Modules:
  0.0 500.8 jit_solution(3926314647147734163)
XLA Ops:
  0.0 280.1 %qkv.1 = (bf16[8,1024,384]{2,1,0:T(8,128)(2,1)}, bf16[8,1024,256]{2,1,0:T(8,128)(2,1)}, bf16[8,256,128]{2,1,0:T(8,128)(2,1)}, s32[8,8,128]{2,1,0:T(8,128)}, bf16[8,640,3840]{2,1,0:T(8,128)(2,1)}) custom-call(bf16[1024,1280]{1,0:T(8,128)(2,1)} %x_ref.1, bf16[640,3840]{1,0:T(8,128)(2,1)} %w_ref.2, s32[8,128]{1,0:T(8,128)} %bitcast.10), custom_call_target="tpu_custom_call" | custom-call | tf_op jit(solution)/shard_map/qkv/pallas_call | solution.py:481
  280.1 1.0 convert_reduce_fusion
  281.1 0.7 pad_add_fusion.tab
  281.8 109.3 %attention.1 = (bf16[8192,128]{1,0:T(8,128)(2,1)}, bf16[2048,128]{1,0:T(8,128)(2,1)}) custom-call(s32[4]{0:T(128)} %pad_add_fusion.tab, bf16[8192,384]{1,0:T(8,128)(2,1)} %bitcast.6, bf16[8192,256]{1,0:T(8,128)(2,1)} %bitcast.7, bf16[2048,128]{1,0:T(8,128)(2,1)} %bitcast.8), custom_call_target="tpu_custom_call" | custom-call | tf_op jit(solution)/shard_map/attention/pallas_call | solution.py:513
  391.1 106.4 %out.1 = bf16[1024,1280]{1,0:T(8,128)(2,1)} custom-call(bf16[8192,128]{1,0:T(8,128)(2,1)} %get-tuple-element.15.o_ref, bf16[2048,128]{1,0:T(8,128)(2,1)} %get-tuple-element.16.so_ref, bf16[640,1280]{1,0:T(8,128)(2,1)} %w_ref.3), custom_call_target="tpu_custom_call" | custom-call | tf_op jit(solution)/shard_map/out/pallas_call | solution.py:533
  497.4 3.4 copy.6
  (1 shorter events, 0.0 us)

commit v2 on v1

--- a/solution.py
+++ b/solution.py
@@ -273,11 +273,11 @@
     weight.drain()
 
 
-def attention_kernel(scale, parts, n_main, tab, m_ref, skv_ref, sq_ref, o_ref, so_ref, vt, svt, exps, tops):
+def attention_kernel(scale, parts, n_main, tab, m_ref, skv_ref, sq_ref, o_ref, so_ref, vt, svt, scores, exps, probs,
+                     tops):
     step = pl.program_id(0)
     seq = m_ref.shape[0]
-    q_tile = o_ref.shape[0]
-    k_tile = 2 * q_tile
+    _, k_tile, _ = exps.shape
     n_bounds = tab.shape[0] - 1
     coef = scale * 1.4426950408889634
     lowest = -0.7 * float(jnp.finfo(jnp.float32).max)
@@ -297,48 +297,69 @@
         return start
 
     def attend(q, k_ref, k_col, vt_ref, row0, out):
+        q_tile = q.shape[0]
+        lanes = slice(0, q_tile)
         row = row0 + lax.broadcasted_iota(jnp.int32, (1, q_tile), 1)
         start = doc_start(row)
         first = doc_start(row0) // k_tile
-        diagonal = row0 // k_tile
+        last = row0 // k_tile
         clear = (doc_start(row0 + q_tile - 1) + k_tile - 1) // k_tile
-        clear = jnp.minimum(clear, diagonal)
-
-        def body(masked, j, carry):
+        clear = jnp.minimum(clear, last)
+
+        def score(j):
+            r = pl.ds(pl.multiple_of(j * k_tile, k_tile), k_tile)
+            scores[:, lanes] = lax.dot_general(k_ref[r, k_col:k_col + HEAD_DIM], q, (((1,), (1,)), ((), ())),
+                                               preferred_element_type=jnp.float32)
+
+        def body(edge, j, carry):
             top, total = carry
-            r = pl.ds(pl.multiple_of(j * k_tile, k_tile), k_tile)
-            s = lax.dot_general(k_ref[r, k_col:k_col + HEAD_DIM], q, (((1,), (1,)), ((), ())),
-                                preferred_element_type=jnp.float32)
-            if masked:
+            s = scores[:, lanes]
+            if edge != "last":
+                score(j + 1)
+            if edge:
                 key = j * k_tile + lax.broadcasted_iota(jnp.int32, s.shape, 0)
-                s = jnp.where((key >= start) & (key <= row), s, lowest)
+                seen = key >= start
+                if edge == "last":
+                    seen &= key <= row
+                s = jnp.where(seen, s, lowest)
             new = jnp.maximum(top, jnp.max(s, axis=0, keepdims=True))
             e = jnp.exp2((s - new) * coef)
-            exps[j] = e
-            tops[j] = new
+            exps[j, :, lanes] = e
+            tops[j, :, lanes] = new
             total = total * jnp.exp2((top - new) * coef) + jnp.sum(e, axis=0, keepdims=True)
             return new, total
 
+        carry = (jnp.full((1, q_tile), lowest, jnp.float32), jnp.zeros((1, q_tile), jnp.float32))
+        score(first)
+        carry = lax.fori_loop(first, clear, functools.partial(body, "first"), carry)
+        carry = lax.fori_loop(clear, last, functools.partial(body, ""), carry)
+        top, total = body("last", last, carry)
+        inverse = 1.0 / total
+
+        def prob(j):
+            share = jnp.exp2((tops[j, :, lanes] - top) * coef) * inverse
+            return (exps[j, :, lanes] * share).astype(jnp.bfloat16)
+
         def weigh(j, o):
-            share = jnp.exp2((tops[j] - top) * coef) / total
-            prob = (exps[j] * share).astype(jnp.bfloat16)
-            return o + jnp.dot(vt_ref[j], prob, preferred_element_type=jnp.float32)
-
-        carry = (jnp.full((1, q_tile), lowest, jnp.float32), jnp.zeros((1, q_tile), jnp.float32))
-        carry = lax.fori_loop(first, clear, functools.partial(body, True), carry)
-        carry = lax.fori_loop(clear, diagonal, functools.partial(body, False), carry)
-        top, total = body(True, diagonal, carry)
-        o = lax.fori_loop(first, diagonal + 1, weigh, jnp.zeros((HEAD_DIM, q_tile), jnp.float32))
+            p = probs[:, lanes]
+            probs[:, lanes] = prob(j + 1)
+            return o + jnp.dot(vt_ref[j], p, preferred_element_type=jnp.float32)
+
+        probs[:, lanes] = prob(first)
+        o = lax.fori_loop(first, last, weigh, jnp.zeros((HEAD_DIM, q_tile), jnp.float32))
+        o = o + jnp.dot(vt_ref[last], probs[:, lanes], preferred_element_type=jnp.float32)
         out[...] = o.T.astype(out.dtype)
 
     @pl.when(step < n_main)
     def _():
+        q_tile = o_ref.shape[0]
         row0 = step * q_tile
         q = m_ref[pl.ds(pl.multiple_of(row0, q_tile), q_tile), :HEAD_DIM]
         attend(q, m_ref, HEAD_DIM, vt, row0, o_ref)
 
     @pl.when(step >= n_main)
     def _():
+        q_tile = so_ref.shape[0]
         i = step - n_main
         row0 = (i * parts + tab[n_bounds]) * q_tile
         q = sq_ref[pl.ds(pl.multiple_of(i * q_tile, q_tile), q_tile), :]
@@ -505,7 +526,8 @@
         starts = jnp.sum((seg_all.reshape(1, seq) < jnp.arange(1, n_docs, dtype=seg_all.dtype)[:, None]).astype(jnp.int32),
                          axis=1)
         table = jnp.concatenate([starts, (lax.axis_index("sp") % parts).astype(jnp.int32)[None]])
-        n_main = seq // q_rows
+        q_tile = k_tile = 2 * q_rows
+        n_main, n_side, n_keys = seq // q_tile, n_sp, seq // k_tile
 
         def whole(shape):
             return pl.BlockSpec(shape, lambda i, t: (0, 0), pipeline_mode=pl.Buffered(1))
@@ -515,13 +537,17 @@
             out_shape=(jax.ShapeDtypeStruct((seq, HEAD_DIM), bf16), jax.ShapeDtypeStruct((seq // parts, HEAD_DIM), bf16)),
             grid_spec=pltpu.PrefetchScalarGridSpec(
                 num_scalar_prefetch=1,
-                grid=(n_main + n_main // parts,),
+                grid=(n_main + n_side,),
                 in_specs=[whole((seq, head)), whole((seq, 2 * HEAD_DIM)), whole((seq // parts, HEAD_DIM))],
-                out_specs=(pl.BlockSpec((q_rows, HEAD_DIM), lambda i, t: (jnp.minimum(i, n_main - 1), 0)),
+                out_specs=(pl.BlockSpec((q_tile, HEAD_DIM), lambda i, t: (jnp.minimum(i, n_main - 1), 0)),
                            pl.BlockSpec((q_rows, HEAD_DIM), lambda i, t: (jnp.maximum(i - n_main, 0), 0))),
-                scratch_shapes=[pltpu.VMEM((seq // (2 * q_rows), HEAD_DIM, 2 * q_rows), bf16)] * 2 + [
-                    pltpu.VMEM((seq // (2 * q_rows), 2 * q_rows, q_rows), jnp.float32),
-                    pltpu.VMEM((seq // (2 * q_rows), 1, q_rows), jnp.float32),
+                scratch_shapes=[
+                    pltpu.VMEM((n_keys, HEAD_DIM, k_tile), bf16),
+                    pltpu.VMEM((n_keys, HEAD_DIM, k_tile), bf16),
+                    pltpu.VMEM((k_tile, q_tile), jnp.float32),
+                    pltpu.VMEM((n_keys, k_tile, q_tile), jnp.float32),
+                    pltpu.VMEM((k_tile, q_tile), bf16),
+                    pltpu.VMEM((n_keys, 1, q_tile), jnp.float32),
                 ],
             ),
             compiler_params=pltpu.CompilerParams(dimension_semantics=("arbitrary",), vmem_limit_bytes=VMEM_LIMIT),

time: 506 us -> 475 us (0.939)
  Pallas kernels: 496 us -> 462 us
    pallas_call x1, Pallas kernels: 109 us -> 71 us  [local_block(): pl.pallas_call(functools.partial(attention_kernel, 1.0 / HEAD_DIM ** 0.5,...]
where the time goes in v2:
time: 475 us; the launch traced here: 467 us
  Pallas kernels  462 us (97%)
    pallas_call x1, Pallas kernels, local_block(): pl.pallas_call(functools.partial(qkv_kernel, n_tp, n_sp), out_shape=(jax....  280 us
    pallas_call x1, Pallas kernels, local_block(): pl.pallas_call(functools.partial(out_kernel, n_tp, n_sp), out_shape=jax.S...  111 us
    pallas_call x1, Pallas kernels, local_block(): pl.pallas_call(functools.partial(attention_kernel, 1.0 / HEAD_DIM ** 0.5,...  71 us

profile of v2, /device:TPU:97, one launch (start us, length us, event | category | flops | bytes accessed | tf_op | source)
XLA Modules:
  0.0 467.0 jit_solution(5734644581184361038)
XLA Ops:
  0.0 280.1 %qkv.1 = (bf16[8,1024,384]{2,1,0:T(8,128)(2,1)}, bf16[8,1024,256]{2,1,0:T(8,128)(2,1)}, bf16[8,256,128]{2,1,0:T(8,128)(2,1)}, s32[8,8,128]{2,1,0:T(8,128)}, bf16[8,640,3840]{2,1,0:T(8,128)(2,1)}) custom-call(bf16[1024,1280]{1,0:T(8,128)(2,1)} %x_ref.1, bf16[640,3840]{1,0:T(8,128)(2,1)} %w_ref.2, s32[8,128]{1,0:T(8,128)} %bitcast.10), custom_call_target="tpu_custom_call" | custom-call | tf_op jit(solution)/shard_map/qkv/pallas_call | solution.py:502
  280.1 1.0 convert_reduce_fusion
  281.1 0.7 pad_add_fusion.tab
  281.8 71.0 %attention.1 = (bf16[8192,128]{1,0:T(8,128)(2,1)}, bf16[2048,128]{1,0:T(8,128)(2,1)}) custom-call(s32[4]{0:T(128)} %pad_add_fusion.tab, bf16[8192,384]{1,0:T(8,128)(2,1)} %bitcast.6, bf16[8192,256]{1,0:T(8,128)(2,1)} %bitcast.7, bf16[2048,128]{1,0:T(8,128)(2,1)} %bitcast.8), custom_call_target="tpu_custom_call" | custom-call | tf_op jit(solution)/shard_map/attention/pallas_call | solution.py:535
  352.8 110.9 %out.1 = bf16[1024,1280]{1,0:T(8,128)(2,1)} custom-call(bf16[8192,128]{1,0:T(8,128)(2,1)} %get-tuple-element.15.o_ref, bf16[2048,128]{1,0:T(8,128)(2,1)} %get-tuple-element.16.so_ref, bf16[640,1280]{1,0:T(8,128)(2,1)} %w_ref.3), custom_call_target="tpu_custom_call" | custom-call | tf_op jit(solution)/shard_map/out/pallas_call | solution.py:559
  463.6 3.4 copy.6
  (1 shorter events, 0.0 us)

commit v3 on v1

v3 whole, which is shorter than its diff:
```python
import functools

import jax
import jax.numpy as jnp
from jax import lax
from jax.experimental import pallas as pl
from jax.experimental.pallas import tpu as pltpu
from jax.sharding import PartitionSpec as P

HEAD_DIM = 128
MESH = pl.DeviceIdType.MESH
ANY = pl.ANY
VMEM_LIMIT = 67_043_328


class Place:
    def __init__(self, n_tp, n_sp):
        self.n_tp, self.n_sp, self.n_x = n_tp, n_sp, n_sp // 2
        self.tp, self.sp = lax.axis_index("tp"), lax.axis_index("sp")
        self.chip, self.core = self.sp // 2, self.sp % 2
        self.sib = self.chip * 2 + 1 - self.core
        self.up, self.down = (self.tp + 1) % n_tp, (self.tp + n_tp - 1) % n_tp
        self.right, self.left = self.at(1, 0), self.at(-1, 0)

    def chip_at(self, r):
        return (self.chip + r + self.n_x) % self.n_x

    def at(self, r, d):
        return self.chip_at(r) * 2 + (self.core if d == 0 else 1 - self.core)

    def barrier(self):
        sem = pltpu.get_barrier_semaphore()
        for j in range(1, self.n_sp):
            pl.semaphore_signal(sem, inc=1, device_id={"sp": (self.sp + j) % self.n_sp}, device_id_type=MESH)
        for peer in (self.up, self.down):
            pl.semaphore_signal(sem, inc=1, device_id={"tp": peer}, device_id_type=MESH)
        pl.semaphore_wait(sem, self.n_sp + 1)


def remote(src, dst, send, recv, **peer):
    return pltpu.make_async_remote_copy(
        src_ref=src, dst_ref=dst, send_sem=send, recv_sem=recv, device_id=peer, device_id_type=MESH
    )


class Ring:
    HALF = (0, 1, 0, 1, 0, 1)

    def __init__(self, axis, me, ahead, behind, far, own, slots, rows, send, recv):
        self.half = (pl.ds(0, rows // 2), pl.ds(rows // 2, rows // 2))
        self.axis, self.me, self.ahead, self.behind, self.far = axis, me, ahead, behind, far
        self.own, self.slots, self.send, self.recv = own, slots, send, recv

    def copy(self, k):
        h = self.half[self.HALF[k]]
        if k in (2, 5):
            src = dst = self.landed(k - 2)
        else:
            src, dst = self.own.at[h], self.slots(self.me).at[h]
        peer = self.ahead if k < 3 else self.behind
        return remote(src, dst, self.send.at[k], self.recv.at[k], **{self.axis: peer})

    def landed(self, k):
        origin = (self.behind, self.behind, self.far, self.ahead, self.ahead, self.far)[k]
        return self.slots(origin).at[self.half[self.HALF[k]]]

    def start(self, *ks):
        for k in ks or (0, 3, 1, 4):
            self.copy(k).start()

    def forward(self):
        for k in (0, 3):
            self.copy(k).wait_recv()
            self.copy(k + 2).start()

    def wait(self, *ks):
        for k in ks:
            self.copy(k).wait_recv()

    def drain(self):
        for k in range(6):
            self.copy(k).wait_send()


class WeightGather:
    def __init__(self, p, own, slots, rows, send, recv, sib_send, sib_recv):
        self.p, self.send, self.recv = p, sib_send, sib_recv
        self.ring = Ring("sp", p.sp, p.right, p.left, p.at(2, 0), own, slots, rows, send, recv)
        self.own = remote(own, slots(p.sp), sib_send.at[6], sib_recv.at[6], sp=p.sib)

    def to_sibling(self, k):
        block = self.ring.landed(k)
        return remote(block, block, self.send.at[k], self.recv.at[k], sp=self.p.sib)

    def forward(self):
        self.ring.forward()
        self.share(0, 3)

    def share(self, *ks):
        for k in ks:
            self.to_sibling(k).start()

    def wait_sibling(self, *ks):
        for k in ks:
            self.to_sibling(k).wait_recv()

    def drain(self):
        self.ring.drain()
        self.own.wait_send()
        for k in range(6):
            self.to_sibling(k).wait_send()


LOWEST = -0.7 * 3.4028235e38
APART = 1e38


def attend(coef, q, keys, values_t, row0, last, scores, exps, probs, tops):
    q_tile = q.shape[0]
    k_tile = scores.shape[0]
    lanes = slice(0, q_tile)

    def score(j):
        scores[:, lanes] = lax.dot_general(keys(j), q, (((1,), (1,)), ((), ())), preferred_element_type=jnp.float32)

    def body(edge, j, carry):
        top, total = carry
        s = scores[:, lanes]
        if not edge:
            score(j + 1)
        else:
            key = j * k_tile + lax.broadcasted_iota(jnp.int32, s.shape, 0)
            row = row0 + lax.broadcasted_iota(jnp.int32, s.shape, 1)
            s = jnp.where(key <= row, s, LOWEST)
        new = jnp.maximum(top, jnp.max(s, axis=0, keepdims=True))
        e = jnp.exp2((s - new) * coef)
        exps[j, :, lanes] = e
        tops[j, :, lanes] = new
        total = total * jnp.exp2((top - new) * coef) + jnp.sum(e, axis=0, keepdims=True)
        return new, total

    carry = (jnp.full((1, q_tile), LOWEST, jnp.float32), jnp.zeros((1, q_tile), jnp.float32))
    score(0)
    carry = lax.fori_loop(0, last, functools.partial(body, False), carry)
    top, total = body(True, last, carry)
    inverse = 1.0 / total

    def prob(j):
        share = jnp.exp2((tops[j, :, lanes] - top) * coef) * inverse
        return (exps[j, :, lanes] * share).astype(jnp.bfloat16)

    def weigh(j, o):
        p = probs[:, lanes]
        probs[:, lanes] = prob(j + 1)
        return o + jnp.dot(values_t[j], p, preferred_element_type=jnp.float32)

    probs[:, lanes] = prob(0)
    o = lax.fori_loop(0, last, weigh, jnp.zeros((HEAD_DIM, q_tile), jnp.float32))
    return o + jnp.dot(values_t[last], probs[:, lanes], preferred_element_type=jnp.float32)


def beside_docs(q, docs):
    return jnp.concatenate([q, ((docs.astype(jnp.float32) - 1.0) * APART).astype(q.dtype)], axis=1)


def qkv_kernel(n_tp, n_sp, coef, x_ref, w_ref, seg_ref, o_out, docs_out, skv, sq, w_all,
               x_all, acc, qkv, w_tile, seg_all, m_all, values_t, docs, o_all, scores, exps, probs, tops,
               local_sem, tile_sem, x_send, x_recv, w_send, w_recv, w_sib_send, w_sib_recv, seg_send, seg_recv,
               main_send, main_recv, kv_send, kv_recv, q_send, q_recv, own_sem, o_sem):
    p = Place(n_tp, n_sp)
    rows, x_cols = x_ref.shape
    w_rows = w_ref.shape[0]
    n_main, _, tile = acc.shape
    n_tiles = n_main + 1
    head = 3 * HEAD_DIM
    n_shared = 2 * n_tiles - n_sp
    parts = n_sp // n_shared
    q_rows = rows // parts
    m_tile = min(rows, 256)
    n_keys, k_tile, q_tile = exps.shape
    seq = n_sp * rows
    n_docs = 4
    p.barrier()

    x_own = pltpu.make_async_copy(x_ref, x_all.at[p.tp], local_sem.at[0])
    x_own.start()
    seg_own = pltpu.make_async_copy(seg_ref, seg_all.at[p.sp], local_sem.at[1])
    seg_own.start()
    x_ring = Ring("tp", p.tp, p.up, p.down, (p.tp + 2) % n_tp, x_ref, lambda i: x_all.at[i], rows, x_send, x_recv)

    def gather(g):
        c = pl.ds(0, n_main * tile) if g == 0 else pl.ds(n_main * tile, tile)
        return WeightGather(p, w_ref.at[:, c], lambda i: w_all.at[i, :, c], w_rows, w_send.at[g], w_recv.at[g],
                            w_sib_send.at[g], w_sib_recv.at[g])

    mains, shared = gather(0), gather(1)
    mains.ring.start()
    x_ring.start()
    mains.own.start()
    shared.own.start()
    seg_copies = []
    for j in range(1, n_sp):
        copy = remote(seg_ref, seg_all.at[p.sp], seg_send.at[j - 1], seg_recv.at[j - 1], sp=(p.sp + j) % n_sp)
        copy.start()
        seg_copies.append(copy)

    def tile_load(w_src, t, slot):
        return pltpu.make_async_copy(
            w_src.at[:, pl.ds(pl.multiple_of(t * tile, tile), tile)], w_tile.at[slot], tile_sem.at[slot])

    def product(shard, m, slot):
        r = pl.ds(pl.multiple_of(m * m_tile, m_tile), m_tile)
        c = pl.ds(pl.multiple_of((shard % 2) * w_rows, w_rows), w_rows)
        return r, jnp.dot(x_all[shard // 2, r, c], w_tile[slot], preferred_element_type=jnp.float32)

    def source(shard, own=False):
        return w_ref if own else w_all.at[shard]

    def accumulate(w_src, shard, first=False):
        tile_load(w_src, 0, 0).start()

        @pl.loop(0, n_main)
        def _(t):
            slot = t % 2
            tile_load(w_src, t, slot).wait()

            @pl.when(t + 1 < n_main)
            def _():
                tile_load(w_src, t + 1, 1 - slot).start()

            @pl.loop(0, rows // m_tile)
            def _(m):
                r, d = product(shard, m, slot)
                if first:
                    acc[t, r] = d
                else:
                    acc[t, r] += d

    x_ring.forward()
    mains.forward()
    x_ring.wait(1, 4, 2, 5)
    mains.ring.wait(1, 4)
    mains.share(1, 4)
    x_own.wait()
    accumulate(w_ref, p.sp, first=True)
    mains.own.wait_recv()
    accumulate(w_all.at[p.sib], p.sib)
    accumulate(w_all.at[p.left], p.left)
    accumulate(w_all.at[p.right], p.right)
    mains.wait_sibling(0, 1)
    accumulate(w_all.at[p.at(-1, 1)], p.at(-1, 1))
    mains.wait_sibling(3, 4)
    accumulate(w_all.at[p.at(1, 1)], p.at(1, 1))
    shared.ring.start(0, 3)
    mains.ring.wait(2, 5)
    mains.share(2, 5)
    accumulate(w_all.at[p.at(2, 0)], p.at(2, 0))
    mains.wait_sibling(2, 5)

    last = p.at(2, 1)
    offsets = (2, 1, -1, 0)
    main_copies = []
    tile_load(w_all.at[last], p.chip_at(2), 0).start()
    for i, r in enumerate(offsets):
        t, slot = p.chip_at(r), i % 2
        tile_load(w_all.at[last], t, slot).wait()
        if i + 1 < n_main:
            tile_load(w_all.at[last], p.chip_at(offsets[i + 1]), 1 - slot).start()

        @pl.loop(0, rows // m_tile)
        def _(m):
            rr, d = product(last, m, slot)
            qkv[t, rr] = (acc[t, rr] + d).astype(qkv.dtype)

        for d in (0, 1):
            core = p.core if d == 0 else 1 - p.core
            src = qkv.at[t, :, pl.ds(pl.multiple_of(core * head, head), head)]
            if r == 0 and d == 0:
                copy = pltpu.make_async_copy(src, m_all.at[p.sp], own_sem.at[0])
            else:
                j = (r % 4) * 2 + d
                copy = remote(src, m_all.at[p.sp], main_send.at[j], main_recv.at[j], sp=p.at(r, d))
            copy.start()
            main_copies.append((copy, r == 0 and d == 0))

    shared.ring.start(1, 4)
    shared.forward()

    def accumulate_shared(a, b, a_own=False, step=0):
        for slot, (shard, own) in enumerate(((a, a_own), (b, False))):
            tile_load(source(shard, own), n_main, slot).start()
        for slot, (shard, own) in enumerate(((a, a_own), (b, False))):
            tile_load(source(shard, own), n_main, slot).wait()

        @pl.loop(0, rows // m_tile)
        def _(m):
            r, d = product(a, m, 0)
            d += product(b, m, 1)[1]
            if step == 0:
                acc[0, r] = d
            elif step == 1:
                acc[0, r] += d
            else:
                qkv[n_main, r] = (acc[0, r] + d).astype(qkv.dtype)

    shared.own.wait_recv()
    accumulate_shared(p.sp, p.sib, a_own=True)

    for copy in seg_copies:
        copy.wait()
    seg_own.wait()
    seg = seg_all[...]
    lane = lax.broadcasted_iota(jnp.int32, (1, HEAD_DIM), 1)
    begin = jnp.zeros((1, HEAD_DIM), jnp.float32)
    end = jnp.where(lane == n_docs - 1, jnp.float32(seq), 0.0)
    for d in range(1, n_docs):
        below = jnp.sum(jnp.where(seg < d, 1.0, 0.0), axis=0)
        below = jnp.sum(jnp.sum(below, axis=0, keepdims=True), axis=1, keepdims=True)
        begin += jnp.where(lane == d, below, 0.0)
        end += jnp.where(lane == d - 1, below, 0.0)

    @pl.loop(0, n_keys)
    def _(j):
        row = (j * k_tile + lax.broadcasted_iota(jnp.int32, (k_tile, HEAD_DIM), 0)).astype(jnp.float32)
        docs[j] = jnp.where((row >= begin) & (row < end), 1.0, 0.0).astype(docs.dtype)

    docs_copy = pltpu.make_async_copy(docs, docs_out, own_sem.at[3])
    docs_copy.start()

    for copy, local in main_copies:
        if local:
            copy.wait()
        else:
            copy.wait_recv()
    per = rows // k_tile

    @pl.loop(0, n_keys)
    def _(j):
        r = pl.ds(pl.multiple_of((j % per) * k_tile, k_tile), k_tile)
        values_t[j] = m_all[j // per, r, 2 * HEAD_DIM:].T

    def keys(j):
        r = pl.ds(pl.multiple_of((j % per) * k_tile, k_tile), k_tile)
        return jnp.concatenate([m_all[j // per, r, HEAD_DIM:2 * HEAD_DIM], docs[j]], axis=1)

    def o_copy(i):
        r = pl.ds(pl.multiple_of(i * q_tile, q_tile), q_tile)
        return pltpu.make_async_copy(o_all.at[r], o_out.at[r], o_sem.at[i])

    def main_attention(lo, hi):
        @pl.loop(lo, hi)
        def _(i):
            r = pl.ds(pl.multiple_of((i % per) * k_tile, k_tile), k_tile)
            q = beside_docs(m_all[i // per, r, :HEAD_DIM], docs[i])
            o = attend(coef, q, keys, values_t, i * q_tile, i, scores, exps, probs, tops)
            o_all[pl.ds(pl.multiple_of(i * q_tile, q_tile), q_tile)] = o.T.astype(o_all.dtype)
            o_copy(i).start()

    early = n_keys - 3
    main_attention(early, n_keys)

    shared.ring.wait(1, 4, 2, 5)
    shared.share(1, 4, 2, 5)
    shared.wait_sibling(0, 1)
    accumulate_shared(p.left, p.at(-1, 1), step=1)
    shared.wait_sibling(3, 4)
    accumulate_shared(p.right, p.at(1, 1), step=1)
    shared.wait_sibling(2, 5)
    accumulate_shared(p.at(2, 0), p.at(2, 1), step=2)

    shared_copies = []
    t = n_main
    for r in (2, 1, -1, 0):
        base = (p.chip_at(r) * 2 // parts) * head
        kv_src = qkv.at[t, :, pl.ds(pl.multiple_of(base + HEAD_DIM, HEAD_DIM), 2 * HEAD_DIM)]
        k = r % 4
        if r == 0:
            copy = pltpu.make_async_copy(kv_src, skv.at[p.sp], own_sem.at[1])
            copy.start()
            shared_copies.append((copy, True))
        copy = remote(kv_src, skv.at[p.sp], kv_send.at[k], kv_recv.at[k], sp=p.sib if r == 0 else p.at(r, 0))
        copy.start()
        shared_copies.append((copy, False if r == 0 else None))
        for d in (0, 1):
            dst = p.at(r, d)
            q_src = qkv.at[t, pl.ds(pl.multiple_of((dst % parts) * q_rows, q_rows), q_rows),
                           pl.ds(pl.multiple_of(base, HEAD_DIM), HEAD_DIM)]
            if r == 0 and d == 0:
                copy = pltpu.make_async_copy(q_src, sq.at[p.sp], own_sem.at[2])
            else:
                j = k * 2 + d
                copy = remote(q_src, sq.at[p.sp], q_send.at[j], q_recv.at[j], sp=dst)
            copy.start()
            shared_copies.append((copy, r == 0 and d == 0))

    main_attention(0, early)

    relays = []
    for r in (1, -1, 2):
        k = r % 4
        arrived = skv.at[p.at(-r, 0)]
        remote(arrived, arrived, kv_send.at[k], kv_recv.at[k], sp=p.at(r, 0)).wait_recv()
        relay = remote(arrived, arrived, kv_send.at[3 + k], kv_recv.at[3 + k], sp=p.sib)
        relay.start()
        relays.append(relay)
    for copy, local in shared_copies:
        if local:
            copy.wait()
        else:
            copy.wait_send()
            if local is False:
                copy.wait_recv()
    for relay in relays:
        relay.wait()
    for copy, local in main_copies:
        if not local:
            copy.wait_send()
    for i in range(n_keys):
        o_copy(i).wait()
    docs_copy.wait()
    x_ring.drain()
    mains.drain()
    shared.drain()


def out_kernel(n_tp, n_sp, coef, o_ref, docs_ref, skv_ref, sq_ref, w_ref, y_ref, ctx, w_all, acc, skv, sq, docs,
               values_t, so_all, scores, exps, probs, tops, local_sem, w_send, w_recv, w_sib_send, w_sib_recv,
               o_send, o_recv, s_send, s_recv, c_send, c_recv):
    p = Place(n_tp, n_sp)
    n_x = p.n_x
    _, rows, local = ctx.shape
    w_rows = w_ref.shape[0]
    n_shared = local // HEAD_DIM - n_sp
    parts = n_sp // n_shared
    q_rows = rows // parts
    m_tile = min(rows, 256)
    pair = 2 * HEAD_DIM
    n_keys, k_tile, _ = exps.shape
    per = rows // k_tile

    loads = [pltpu.make_async_copy(src, dst, local_sem.at[3 + i])
             for i, (src, dst) in enumerate(((skv_ref, skv), (sq_ref, sq), (docs_ref, docs)))]
    for load in loads:
        load.start()
    w_own = pltpu.make_async_copy(w_ref, w_all.at[p.sp], local_sem.at[0])
    w_own.start()
    p.barrier()

    def head_copy(r, d):
        dst = p.at(r, d)
        src = o_ref.at[pl.ds(pl.multiple_of(dst * rows, rows), rows)]
        to = ctx.at[p.tp, :, pl.ds(pl.multiple_of(p.sp * HEAD_DIM, HEAD_DIM), HEAD_DIM)]
        if r == 0 and d == 0:
            return pltpu.make_async_copy(src, to, local_sem.at[1])
        j = (r % 4) * 2 + d
        return remote(src, to, o_send.at[j], o_recv.at[j], sp=dst)

    def shared_copy(r, d):
        dst = p.at(r, d)
        src = so_all.at[pl.ds(pl.multiple_of(dst * q_rows, q_rows), q_rows)]
        to = ctx.at[p.tp, pl.ds(pl.multiple_of((p.sp % parts) * q_rows, q_rows), q_rows),
                    pl.ds(pl.multiple_of((n_sp + p.sp // parts) * HEAD_DIM, HEAD_DIM), HEAD_DIM)]
        if r == 0 and d == 0:
            return pltpu.make_async_copy(src, to, local_sem.at[2])
        j = (r % 4) * 2 + d
        return remote(src, to, s_send.at[j], s_recv.at[j], sp=dst)

    peers = [(r, d) for r in (0, 1, -1, 2) for d in (0, 1)]
    for r, d in peers:
        head_copy(r, d).start()
    weight = WeightGather(p, w_ref, lambda i: w_all.at[i], w_rows, w_send, w_recv, w_sib_send, w_sib_recv)
    weight.ring.start(0, 3)
    weight.own.start()

    def ring(i, column):
        c = pl.ds(pl.multiple_of(column, pair), pair)
        return Ring("tp", p.tp, p.up, p.down, (p.tp + 2) % n_tp, ctx.at[p.tp, :, c], lambda j: ctx.at[j, :, c], rows,
                    c_send.at[i], c_recv.at[i])

    def wait_in(copy, local):
        if local:
            copy.wait()
        else:
            copy.wait_recv()

    rings = []

    def start_ring(i, r):
        for d in (0, 1):
            wait_in(head_copy(r, d), r == 0 and d == 0)
        rings.append(ring(i, p.chip_at(-r) * pair))
        rings[-1].start()

    def keys(j):
        r = pl.ds(pl.multiple_of((j % per) * k_tile, k_tile), k_tile)
        return jnp.concatenate([skv[j // per, r, :HEAD_DIM], docs[j]], axis=1)

    def shared_attention(lo, hi):
        @pl.loop(lo, hi)
        def _(i):
            row0 = (i * parts + p.sp % parts) * q_rows
            j = row0 // k_tile
            r = pl.ds(pl.multiple_of(row0 % k_tile, q_rows), q_rows)
            q = beside_docs(sq[i], docs[j, r])
            o = attend(coef, q, keys, values_t, row0, j, scores, exps, probs, tops)
            so_all[pl.ds(pl.multiple_of(i * q_rows, q_rows), q_rows)] = o.T.astype(so_all.dtype)

    start_ring(0, 0)
    for load in loads:
        load.wait()

    @pl.loop(0, n_keys)
    def _(j):
        r = pl.ds(pl.multiple_of((j % per) * k_tile, k_tile), k_tile)
        values_t[j] = skv[j // per, r, HEAD_DIM:].T

    shared_attention(0, n_sp // 2)
    start_ring(1, 1)
    start_ring(2, -1)
    shared_attention(n_sp // 2, n_sp)
    for r, d in peers:
        shared_copy(r, d).start()
    weight.ring.start(1, 4)
    start_ring(3, 2)
    rings[0].forward()
    rings[1].forward()
    rings[2].forward()
    weight.forward()
    for r, d in peers:
        wait_in(shared_copy(r, d), r == 0 and d == 0)
    rings.append(ring(n_x, n_sp * HEAD_DIM))
    rings[-1].start()
    for c in rings[3:]:
        c.forward()
    weight.ring.wait(1, 4)
    weight.share(1, 4)
    for c in rings:
        c.wait(1, 4)
    w_own.wait()
    weight.own.wait_recv()
    weight.wait_sibling(0, 1, 3, 4)

    def block(j, step):
        @pl.loop(0, rows // m_tile)
        def _(m):
            r = pl.ds(pl.multiple_of(m * m_tile, m_tile), m_tile)
            d = jnp.dot(ctx[j, r, :w_rows], w_all[2 * j], preferred_element_type=jnp.float32)
            d += jnp.dot(ctx[j, r, w_rows:], w_all[2 * j + 1], preferred_element_type=jnp.float32)
            if step == 0:
                acc[r] = d
            elif step < n_tp - 1:
                acc[r] += d
            else:
                y_ref[r] = (acc[r] + d).astype(y_ref.dtype)

    turn = (p.chip + n_x - p.tp) % n_x
    far = turn // 2
    block((p.tp + far * (1 - turn % 2)) % n_tp, 0)
    block((p.tp + 1 + 2 * far) % n_tp, 1)
    weight.ring.wait(2, 5)
    weight.share(2, 5)
    weight.wait_sibling(2, 5)
    block((p.tp + far * (turn - 2) + (1 - far) * 3) % n_tp, 2)
    for c in rings:
        c.wait(2, 5)
    block((p.tp + 2) % n_tp, 3)

    for c in rings:
        c.drain()
    weight.drain()
    for r, d in peers:
        if not (r == 0 and d == 0):
            head_copy(r, d).wait_send()
            shared_copy(r, d).wait_send()


def solution(mesh):
    n_tp, n_sp = mesh.shape["tp"], mesh.shape["sp"]
    dma = pltpu.SemaphoreType.DMA
    hbm = pl.BlockSpec(memory_space=ANY)
    coef = 1.0 / HEAD_DIM ** 0.5 * 1.4426950408889634

    def params(collective_id):
        return pltpu.CompilerParams(collective_id=collective_id, has_side_effects=True, vmem_limit_bytes=VMEM_LIMIT)

    def local_block(x_blk, wqkv_blk, wout_blk, seg_blk):
        rows, x_cols = x_blk.shape
        w_rows, n_cols = wqkv_blk.shape
        head = 3 * HEAD_DIM
        heads = n_cols // head
        local = heads * HEAD_DIM
        parts = n_sp // (heads - n_sp)
        q_rows = rows // parts
        tile = 2 * head
        n_tiles = n_cols // tile
        n_main = n_tiles - 1
        seq = n_sp * rows
        q_tile = k_tile = 2 * q_rows
        n_keys = seq // k_tile
        bf16, f32 = x_blk.dtype, jnp.float32
        seg = seg_blk.reshape(rows // 128, 128)

        def attention_scratch(q):
            return [
                pltpu.VMEM((k_tile, q), f32),
                pltpu.VMEM((n_keys, k_tile, q), f32),
                pltpu.VMEM((k_tile, q), bf16),
                pltpu.VMEM((n_keys, 1, q), f32),
            ]

        o_main, docs, skv, sq, _ = pl.pallas_call(
            functools.partial(qkv_kernel, n_tp, n_sp, coef),
            out_shape=(
                jax.ShapeDtypeStruct((seq, HEAD_DIM), bf16),
                jax.ShapeDtypeStruct((n_keys, k_tile, HEAD_DIM), bf16),
                jax.ShapeDtypeStruct((n_sp, rows, 2 * HEAD_DIM), bf16),
                jax.ShapeDtypeStruct((n_sp, q_rows, HEAD_DIM), bf16),
                jax.ShapeDtypeStruct((n_sp, w_rows, n_cols), bf16),
            ),
            in_specs=[hbm] * 3,
            out_specs=(hbm,) * 5,
            scratch_shapes=[
                pltpu.VMEM((n_tp, rows, x_cols), bf16),
                pltpu.VMEM((n_main, rows, tile), f32),
                pltpu.VMEM((n_tiles, rows, tile), bf16),
                pltpu.VMEM((2, w_rows, tile), bf16),
                pltpu.VMEM((n_sp,) + seg.shape, seg.dtype),
                pltpu.VMEM((n_sp, rows, head), bf16),
                pltpu.VMEM((n_keys, HEAD_DIM, k_tile), bf16),
                pltpu.VMEM((n_keys, k_tile, HEAD_DIM), bf16),
                pltpu.VMEM((seq, HEAD_DIM), bf16),
                *attention_scratch(q_tile),
                dma((2,)), dma((2,)), dma((6,)), dma((6,)), dma((2, 6)), dma((2, 6)), dma((2, 7)), dma((2, 7)),
                dma((n_sp - 1,)), dma((n_sp - 1,)), dma((8,)), dma((8,)), dma((7,)), dma((7,)), dma((8,)), dma((8,)),
                dma((4,)), dma((n_keys,)),
            ],
            compiler_params=params(0),
            name="qkv",
        )(x_blk, wqkv_blk, seg)

        wo_rows, wo_cols = wout_blk.shape
        n_rings = local // (2 * HEAD_DIM)
        return pl.pallas_call(
            functools.partial(out_kernel, n_tp, n_sp, coef),
            out_shape=jax.ShapeDtypeStruct((rows, wo_cols), bf16),
            in_specs=[hbm] * 5,
            out_specs=pl.BlockSpec(memory_space=pltpu.VMEM),
            scratch_shapes=[
                pltpu.VMEM((n_tp, rows, local), bf16),
                pltpu.VMEM((n_sp, wo_rows, wo_cols), bf16),
                pltpu.VMEM((rows, wo_cols), f32),
                pltpu.VMEM((n_sp, rows, 2 * HEAD_DIM), bf16),
                pltpu.VMEM((n_sp, q_rows, HEAD_DIM), bf16),
                pltpu.VMEM((n_keys, k_tile, HEAD_DIM), bf16),
                pltpu.VMEM((n_keys, HEAD_DIM, k_tile), bf16),
                pltpu.VMEM((seq // parts, HEAD_DIM), bf16),
                *attention_scratch(q_rows),
                dma((6,)), dma((6,)), dma((6,)), dma((7,)), dma((7,)),
                dma((8,)), dma((8,)), dma((8,)), dma((8,)), dma((n_rings, 6)), dma((n_rings, 6)),
            ],
            compiler_params=params(1),
            name="out",
        )(o_main, docs, skv, sq, wout_blk)

    row_spec = P(("dp", "sp"), "tp")
    return jax.shard_map(
        local_block, mesh=mesh, in_specs=(row_spec, P("sp", "tp"), P("sp", "tp"), P(("dp", "sp"))),
        out_specs=row_spec, check_vma=False)
```

time: 506 us -> 470 us (0.929)
  Pallas kernels: 496 us -> 466 us
    pallas_call x3 -> x2, Pallas kernels: 496 us -> 466 us  [the longest x1 352 us: local_block(): pl.pallas_call(functools.partial(qkv_kernel, n_tp, n_sp, coef), out_shape...]
where the time goes in v3:
time: 470 us; the launch traced here: 469 us
  Pallas kernels  466 us (99%)
    pallas_call x1, Pallas kernels, local_block(): pl.pallas_call(functools.partial(qkv_kernel, n_tp, n_sp, coef), out_shape...  352 us
    pallas_call x1, Pallas kernels, local_block(): pl.pallas_call(functools.partial(out_kernel, n_tp, n_sp, coef), out_shape...  114 us

profile of v3, /device:TPU:97, one launch (start us, length us, event | category | flops | bytes accessed | tf_op | source)
XLA Modules:
  0.0 469.1 jit_solution(13173219825130276127)
XLA Ops:
  0.0 352.1 %qkv.1 = (bf16[8192,128]{1,0:T(8,128)(2,1)}, bf16[16,512,128]{2,1,0:T(8,128)(2,1)}, bf16[8,1024,256]{2,1,0:T(8,128)(2,1)}, bf16[8,256,128]{2,1,0:T(8,128)(2,1)}, bf16[8,640,3840]{2,1,0:T(8,128)(2,1)}) custom-call(bf16[1024,1280]{1,0:T(8,128)(2,1)} %x_ref.1, bf16[640,3840]{1,0:T(8,128)(2,1)} %w_ref.2, s32[8,128]{1,0:T(8,128)} %bitcast.1), custom_call_target="tpu_custom_call" | custom-call | tf_op jit(solution)/shard_map/qkv/pallas_call | solution.py:611
  352.1 113.5 %out.1 = bf16[1024,1280]{1,0:T(8,128)(2,1)} custom-call(bf16[8192,128]{1,0:T(8,128)(2,1)} %get-tuple-element.9.o_ref, bf16[16,512,128]{2,1,0:T(8,128)(2,1)} %get-tuple-element.10.docs_ref, bf16[8,1024,256]{2,1,0:T(8,128)(2,1)} %get-tuple-element.11.skv_ref, bf16[8,256,128]{2,1,0:T(8,128)(2,1)} %get-tuple-element.12.sq_ref, bf16[640,1280]{1,0:T(8,128)(2,1)} %w_ref.3), custom_call_target="tpu_custom_call" | custom-call | tf_op jit(solution)/shard_map/out/pallas_call | solution.py:643
  465.7 3.4 copy.6

commit v4 on v3

--- a/solution.py
+++ b/solution.py
@@ -163,7 +163,7 @@
     return jnp.concatenate([q, ((docs.astype(jnp.float32) - 1.0) * APART).astype(q.dtype)], axis=1)
 
 
-def qkv_kernel(n_tp, n_sp, coef, x_ref, w_ref, seg_ref, o_out, docs_out, skv, sq, w_all,
+def qkv_kernel(n_tp, n_sp, coef, n_done, x_ref, w_ref, seg_ref, o_out, docs_out, m_out, seg_out, skv, sq, w_all,
                x_all, acc, qkv, w_tile, seg_all, m_all, values_t, docs, o_all, scores, exps, probs, tops,
                local_sem, tile_sem, x_send, x_recv, w_send, w_recv, w_sib_send, w_sib_recv, seg_send, seg_recv,
                main_send, main_recv, kv_send, kv_recv, q_send, q_recv, own_sem, o_sem):
@@ -327,11 +327,16 @@
     docs_copy = pltpu.make_async_copy(docs, docs_out, own_sem.at[3])
     docs_copy.start()
 
+    seg_copy = pltpu.make_async_copy(seg_all, seg_out, own_sem.at[4])
+    seg_copy.start()
+
     for copy, local in main_copies:
         if local:
             copy.wait()
         else:
             copy.wait_recv()
+    m_copy = pltpu.make_async_copy(m_all, m_out, own_sem.at[5])
+    m_copy.start()
     per = rows // k_tile
 
     @pl.loop(0, n_keys)
@@ -356,8 +361,8 @@
             o_all[pl.ds(pl.multiple_of(i * q_tile, q_tile), q_tile)] = o.T.astype(o_all.dtype)
             o_copy(i).start()
 
-    early = n_keys - 3
-    main_attention(early, n_keys)
+    early = n_done * 5 // 9
+    main_attention(0, early)
 
     shared.ring.wait(1, 4, 2, 5)
     shared.share(1, 4, 2, 5)
@@ -393,7 +398,7 @@
             copy.start()
             shared_copies.append((copy, r == 0 and d == 0))
 
-    main_attention(0, early)
+    main_attention(early, n_done)
 
     relays = []
     for r in (1, -1, 2):
@@ -415,12 +420,94 @@
     for copy, local in main_copies:
         if not local:
             copy.wait_send()
-    for i in range(n_keys):
+    for i in range(n_done):
         o_copy(i).wait()
     docs_copy.wait()
+    seg_copy.wait()
+    m_copy.wait()
     x_ring.drain()
     mains.drain()
     shared.drain()
+
+
+def tail_kernel(coef, n_done, tab, m_ref, o_in, o_ref, vt, scores, exps, probs, tops):
+    del o_in
+    step = pl.program_id(0)
+    seq = m_ref.shape[0]
+    _, k_tile, _ = exps.shape
+    n_bounds = tab.shape[0]
+
+    @pl.when(step == 0)
+    def _():
+        @pl.loop(0, seq // k_tile)
+        def _(j):
+            r = pl.ds(pl.multiple_of(j * k_tile, k_tile), k_tile)
+            vt[j] = m_ref[r, 2 * HEAD_DIM:].T
+
+    def doc_start(row):
+        start = row * 0
+        for d in range(n_bounds):
+            start = jnp.where(row >= tab[d], tab[d], start)
+        return start
+
+    def attend_tail(q, k_ref, k_col, vt_ref, row0, out):
+        q_tile = q.shape[0]
+        lanes = slice(0, q_tile)
+        row = row0 + lax.broadcasted_iota(jnp.int32, (1, q_tile), 1)
+        start = doc_start(row)
+        first = doc_start(row0) // k_tile
+        last = row0 // k_tile
+        clear = (doc_start(row0 + q_tile - 1) + k_tile - 1) // k_tile
+        clear = jnp.minimum(clear, last)
+
+        def score(j):
+            r = pl.ds(pl.multiple_of(j * k_tile, k_tile), k_tile)
+            scores[:, lanes] = lax.dot_general(k_ref[r, k_col:k_col + HEAD_DIM], q, (((1,), (1,)), ((), ())),
+                                               preferred_element_type=jnp.float32)
+
+        def body(edge, j, carry):
+            top, total = carry
+            s = scores[:, lanes]
+            if edge != "last":
+                score(j + 1)
+            if edge:
+                key = j * k_tile + lax.broadcasted_iota(jnp.int32, s.shape, 0)
+                seen = key >= start
+                if edge == "last":
+                    seen &= key <= row
+                s = jnp.where(seen, s, LOWEST)
+            new = jnp.maximum(top, jnp.max(s, axis=0, keepdims=True))
+            e = jnp.exp2((s - new) * coef)
+            exps[j, :, lanes] = e
+            tops[j, :, lanes] = new
+            total = total * jnp.exp2((top - new) * coef) + jnp.sum(e, axis=0, keepdims=True)
+            return new, total
+
+        carry = (jnp.full((1, q_tile), LOWEST, jnp.float32), jnp.zeros((1, q_tile), jnp.float32))
+        score(first)
+        carry = lax.fori_loop(first, clear, functools.partial(body, "first"), carry)
+        carry = lax.fori_loop(clear, last, functools.partial(body, ""), carry)
+        top, total = body("last", last, carry)
+        inverse = 1.0 / total
+
+        def prob(j):
+            share = jnp.exp2((tops[j, :, lanes] - top) * coef) * inverse
+            return (exps[j, :, lanes] * share).astype(jnp.bfloat16)
+
+        def weigh(j, o):
+            p = probs[:, lanes]
+            probs[:, lanes] = prob(j + 1)
+            return o + jnp.dot(vt_ref[j], p, preferred_element_type=jnp.float32)
+
+        probs[:, lanes] = prob(first)
+        o = lax.fori_loop(first, last, weigh, jnp.zeros((HEAD_DIM, q_tile), jnp.float32))
+        o = o + jnp.dot(vt_ref[last], probs[:, lanes], preferred_element_type=jnp.float32)
+        out[...] = o.T.astype(out.dtype)
+
+    q_tile = o_ref.shape[0]
+    row0 = (step + n_done) * q_tile
+    q = m_ref[pl.ds(pl.multiple_of(row0, q_tile), q_tile), :HEAD_DIM]
+    attend_tail(q, m_ref, HEAD_DIM, vt, row0, o_ref)
 
 
 def out_kernel(n_tp, n_sp, coef, o_ref, docs_ref, skv_ref, sq_ref, w_ref, y_ref, ctx, w_all, acc, skv, sq, docs,
@@ -608,17 +695,20 @@
                 pltpu.VMEM((n_keys, 1, q), f32),
             ]
 
-        o_main, docs, skv, sq, _ = pl.pallas_call(
-            functools.partial(qkv_kernel, n_tp, n_sp, coef),
+        n_done = n_keys * 9 // 16
+        o_main, docs, m_all, seg_all, skv, sq, _ = pl.pallas_call(
+            functools.partial(qkv_kernel, n_tp, n_sp, coef, n_done),
             out_shape=(
                 jax.ShapeDtypeStruct((seq, HEAD_DIM), bf16),
                 jax.ShapeDtypeStruct((n_keys, k_tile, HEAD_DIM), bf16),
+                jax.ShapeDtypeStruct((n_sp, rows, head), bf16),
+                jax.ShapeDtypeStruct((n_sp,) + seg.shape, seg.dtype),
                 jax.ShapeDtypeStruct((n_sp, rows, 2 * HEAD_DIM), bf16),
                 jax.ShapeDtypeStruct((n_sp, q_rows, HEAD_DIM), bf16),
                 jax.ShapeDtypeStruct((n_sp, w_rows, n_cols), bf16),
             ),
             in_specs=[hbm] * 3,
-            out_specs=(hbm,) * 5,
+            out_specs=(hbm,) * 7,
             scratch_shapes=[
                 pltpu.VMEM((n_tp, rows, x_cols), bf16),
                 pltpu.VMEM((n_main, rows, tile), f32),
@@ -632,11 +722,28 @@
                 *attention_scratch(q_tile),
                 dma((2,)), dma((2,)), dma((6,)), dma((6,)), dma((2, 6)), dma((2, 6)), dma((2, 7)), dma((2, 7)),
                 dma((n_sp - 1,)), dma((n_sp - 1,)), dma((8,)), dma((8,)), dma((7,)), dma((7,)), dma((8,)), dma((8,)),
-                dma((4,)), dma((n_keys,)),
+                dma((6,)), dma((n_keys,)),
             ],
             compiler_params=params(0),
             name="qkv",
         )(x_blk, wqkv_blk, seg)
+
+        seg_ids = jnp.arange(1, 4, dtype=seg_all.dtype)[:, None]
+        starts = jnp.sum((seg_all.reshape(1, seq) < seg_ids).astype(jnp.int32), axis=1)
+        o_main = pl.pallas_call(
+            functools.partial(tail_kernel, coef, n_done),
+            out_shape=jax.ShapeDtypeStruct((seq, HEAD_DIM), bf16),
+            grid_spec=pltpu.PrefetchScalarGridSpec(
+                num_scalar_prefetch=1,
+                grid=(n_keys - n_done,),
+                in_specs=[pl.BlockSpec((seq, head), lambda i, t: (0, 0), pipeline_mode=pl.Buffered(1)), hbm],
+                out_specs=pl.BlockSpec((q_tile, HEAD_DIM), lambda i, t: (i + n_done, 0)),
+                scratch_shapes=[pltpu.VMEM((n_keys, HEAD_DIM, k_tile), bf16), *attention_scratch(q_tile)],
+            ),
+            input_output_aliases={2: 0},
+            compiler_params=pltpu.CompilerParams(dimension_semantics=("arbitrary",), vmem_limit_bytes=VMEM_LIMIT),
+            name="tail",
+        )(starts, m_all.reshape(seq, head), o_main)
 
         wo_rows, wo_cols = wout_blk.shape
         n_rings = local // (2 * HEAD_DIM)

time: 470 us -> 446 us (0.949)
  Pallas kernels: 466 us -> 440 us
    pallas_call x1 -> x2, Pallas kernels: 352 us -> 328 us  [the longest x1 299 us: local_block(): pl.pallas_call(functools.partial(qkv_kernel, n_tp, n_sp, coef, n_done), o...]
where the time goes in v4:
time: 446 us; the launch traced here: 445 us
  Pallas kernels  440 us (99%)
    pallas_call x1, Pallas kernels, local_block(): pl.pallas_call(functools.partial(qkv_kernel, n_tp, n_sp, coef, n_done), o...  299 us
    pallas_call x1, Pallas kernels, local_block(): pl.pallas_call(functools.partial(out_kernel, n_tp, n_sp, coef), out_shape...  112 us
    pallas_call x1, Pallas kernels, local_block(): pl.pallas_call(functools.partial(tail_kernel, coef, n_done), out_shape=ja...  29.1 us

profile of v4, /device:TPU:97, one launch (start us, length us, event | category | flops | bytes accessed | tf_op | source)
XLA Modules:
  0.0 444.8 jit_solution(3925281999918988593)
XLA Ops:
  0.0 298.5 %qkv.1 = (bf16[8192,128]{1,0:T(8,128)(2,1)}, bf16[16,512,128]{2,1,0:T(8,128)(2,1)}, bf16[8,1024,384]{2,1,0:T(8,128)(2,1)}, s32[8,8,128]{2,1,0:T(8,128)}, bf16[8,...) custom-call(bf16[1024,1280]{1,0:T(8,128)(2,1)} %x_ref.1, ...), custom_call_target="tpu_custom_call" | custom-call | tf_op jit(solution)/shard_map/qkv/pallas_call | solution.py:699
  298.6 1.5 convert_reduce_fusion.tab
  300.1 29.1 %tail.1.o_ref = bf16[8192,128]{1,0:T(8,128)(2,1)} custom-call(s32[3]{0:T(128)} %convert_reduce_fusion.tab, bf16[8192,384]{1,0:T(8,128)(2,1)} %bitcast.3, bf16[8192,128]{1,0:T(8,128)(2,1)} %get-tuple-element.13.o_in), custom_call_target="tpu_custom_call", output_to_operand_aliasing={{}: (2, {})} | custom-call | tf_op jit(solution)/shard_map/tail/pallas_call | solution.py:733
  329.1 112.2 %out.1 = bf16[1024,1280]{1,0:T(8,128)(2,1)} custom-call(bf16[8192,128]{1,0:T(8,128)(2,1)} %tail.1.o_ref, bf16[16,512,128]{2,1,0:T(8,128)(2,1)} %get-tuple-element.14.docs_ref, bf16[8,1024,256]{2,1,0:T(8,128)(2,1)} %get-tuple-element.15.skv_ref, bf16[8,256,128]{2,1,0:T(8,128)(2,1)} %get-tuple-element.16.sq_ref, bf16[640,1280]{1,0:T(8,128)(2,1)} %w_ref.3), custom_call_target="tpu_custom_call" | custom-call | tf_op jit(solution)/shard_map/out/pallas_call | solution.py:750
  441.4 3.4 copy.8
  (1 shorter events, 0.0 us)

commit v5 on v4

--- a/solution.py
+++ b/solution.py
@@ -361,7 +361,7 @@
             o_all[pl.ds(pl.multiple_of(i * q_tile, q_tile), q_tile)] = o.T.astype(o_all.dtype)
             o_copy(i).start()
 
-    early = n_done * 5 // 9
+    early = n_done * 5 // 7
     main_attention(0, early)
 
     shared.ring.wait(1, 4, 2, 5)
@@ -695,7 +695,7 @@
                 pltpu.VMEM((n_keys, 1, q), f32),
             ]
 
-        n_done = n_keys * 9 // 16
+        n_done = n_keys * 7 // 16
         o_main, docs, m_all, seg_all, skv, sq, _ = pl.pallas_call(
             functools.partial(qkv_kernel, n_tp, n_sp, coef, n_done),
             out_shape=(

time: 446 us -> 457 us (1.025); the launches traced: 445 us -> 462 us
  Pallas kernels: 440 us -> 457 us
    pallas_call x1, Pallas kernels: 29.1 us -> 46.2 us  [local_block(): pl.pallas_call(functools.partial(tail_kernel, coef, n_done), out_shape=ja...]
where the time goes in v5:
time: 457 us; the launch traced here: 462 us
  Pallas kernels  457 us (100%)
    pallas_call x1, Pallas kernels, local_block(): pl.pallas_call(functools.partial(qkv_kernel, n_tp, n_sp, coef, n_done), o...  299 us
    pallas_call x1, Pallas kernels, local_block(): pl.pallas_call(functools.partial(out_kernel, n_tp, n_sp, coef), out_shape...  112 us
    pallas_call x1, Pallas kernels, local_block(): pl.pallas_call(functools.partial(tail_kernel, coef, n_done), out_shape=ja...  46.2 us

profile of v5, /device:TPU:97, one launch (start us, length us, event | category | flops | bytes accessed | tf_op | source)
XLA Modules:
  0.0 461.9 jit_solution(1356438198279038551)
XLA Ops:
  0.0 298.5 %qkv.1 = (bf16[8192,128]{1,0:T(8,128)(2,1)}, bf16[16,512,128]{2,1,0:T(8,128)(2,1)}, bf16[8,1024,384]{2,1,0:T(8,128)(2,1)}, s32[8,8,128]{2,1,0:T(8,128)}, bf16[8,...) custom-call(bf16[1024,1280]{1,0:T(8,128)(2,1)} %x_ref.1, ...), custom_call_target="tpu_custom_call" | custom-call | tf_op jit(solution)/shard_map/qkv/pallas_call | solution.py:699
  298.6 1.5 convert_reduce_fusion.tab
  300.1 46.2 %tail.1.o_ref = bf16[8192,128]{1,0:T(8,128)(2,1)} custom-call(s32[3]{0:T(128)} %convert_reduce_fusion.tab, bf16[8192,384]{1,0:T(8,128)(2,1)} %bitcast.3, bf16[8192,128]{1,0:T(8,128)(2,1)} %get-tuple-element.13.o_in), custom_call_target="tpu_custom_call", output_to_operand_aliasing={{}: (2, {})} | custom-call | tf_op jit(solution)/shard_map/tail/pallas_call | solution.py:733
  346.3 112.2 %out.1 = bf16[1024,1280]{1,0:T(8,128)(2,1)} custom-call(bf16[8192,128]{1,0:T(8,128)(2,1)} %tail.1.o_ref, bf16[16,512,128]{2,1,0:T(8,128)(2,1)} %get-tuple-element.14.docs_ref, bf16[8,1024,256]{2,1,0:T(8,128)(2,1)} %get-tuple-element.15.skv_ref, bf16[8,256,128]{2,1,0:T(8,128)(2,1)} %get-tuple-element.16.sq_ref, bf16[640,1280]{1,0:T(8,128)(2,1)} %w_ref.3), custom_call_target="tpu_custom_call" | custom-call | tf_op jit(solution)/shard_map/out/pallas_call | solution.py:750
  458.5 3.4 copy.8
  (1 shorter events, 0.0 us)
